TPU v7x, 128 devices: a whole 4x4x4 slice. The times are simulated.
128 devices in a mesh: tm: 64 (over y, x, z), batch: 2 (over core).
Axes of the slice: x: 4, y: 4, z: 4, core: 2. Of those that a mesh axis runs over, the one named last changes fastest.
Arguments:
- state_map: float32 [2048, 256, 256], P(('batch', 'tm')), parts along dimension 0, may hold values from -0.375 to 0.375
- input_map: float32 [2048, 64, 256], P(('batch', 'tm')), parts along dimension 0, may hold values from -0.375 to 0.375
- closed_loop: float32 [2048, 256, 256], P(('batch', 'tm')), parts along dimension 0, may hold values from -1.001 to 1.001
- feedback: float32 [2048, 64, 256], P(('batch', 'tm')), parts along dimension 0, may hold values from -0.375 to 0.375
- value_matrix: float32 [2048, 256, 256], P(('batch', 'tm')), parts along dimension 0, may hold values from -0.046875 to 1.5, as said below
- gain_inverse: float32 [2048, 64, 64], P(('batch', 'tm')), parts along dimension 0, may hold values from -0.0105 to 0.2, as said below
- input_weight: float32 [128, 64], P('batch'), parts along dimension 0, may hold values from -0.36 to 6, as said below
- state_weight: float32 [2048, 256], P(('batch', 'tm')), parts along dimension 0, may hold values from 0.1 to 3
- state_linear: float32 [2048, 256], P(('batch', 'tm')), parts along dimension 0, may hold values from -0.18 to 0.18
- input_linear: float32 [2048, 64], P(('batch', 'tm')), parts along dimension 0, may hold values from -0.18 to 0.18
- offset: float32 [2048, 256], P(('batch', 'tm')), parts along dimension 0, may hold values from -0.18 to 0.18
- upper_bound: float32 [2048, 64], P(('batch', 'tm')), parts along dimension 0, may hold values from 0.1 to 0.3
- states: float32 [2048, 256], P(('batch', 'tm')), parts along dimension 0, may hold values from -0.18 to 0.18
- inputs: float32 [2048, 64], P(('batch', 'tm')), parts along dimension 0, may hold values from -0.18 to 0.18
- multipliers: float32 [2048, 256], P(('batch', 'tm')), parts along dimension 0, may hold values from -0.18 to 0.18
- bound_mult: float32 [2048, 64], P(('batch', 'tm')), parts along dimension 0, may hold values from 0 to 0.06
- active: int32 [2048, 64], P(('batch', 'tm')), parts along dimension 0, may hold values 0 or 1
Outputs:
- state_step: float32 [2048, 256], P(('batch', 'tm')), parts along dimension 0
- input_step: float32 [2048, 64], P(('batch', 'tm')), parts along dimension 0
- multiplier_step: float32 [2048, 256], P(('batch', 'tm')), parts along dimension 0
- bound_step: float32 [2048, 64], P(('batch', 'tm')), parts along dimension 0
- kkt_norms: float32 [6], P('batch'), parts along dimension 0
There are 2 independent parts, one for each index of `batch`. A program takes and returns all parts, laid end to end along the dimension named above; each array names one. Nothing has to cross between parts.
Inputs may be any that keep to these rules, and one draw needn't show every extreme that they name: `value_matrix`: each section's matrix is symmetric. `gain_inverse`: each section's matrix is symmetric. `input_weight`: symmetric.
All inputs are finite; a program needn't handle non-finite values. No bound on the sum of `active` on one device may be relied on, other than what follows from the above.
Results may differ from a plain program's by a relative error of at most 0.0003.
Values sent between devices are 32-bit elements; how exact they have to be, the bound alone decides.
No kernel may reach another device: no remote copies, remote signals or barrier semaphores. Data moves between devices by JAX's collectives and lax.ppermute only.
A program may use at most 128 MiB of HBM per device.

v0:
```python
import jax
import jax.numpy as jnp
from jax import lax
from jax.sharding import Mesh
from jax.sharding import PartitionSpec as P

TM = ("tm_0", "tm_1", "tm_2")
BATCH_TM = ("batch", "tm_0", "tm_1", "tm_2")


PRECISE = lax.Precision.HIGHEST
floor_share = 0.001


def shifted(x, axis, by):
    peers = lax.axis_size(axis)
    pairs = [(i, i + by) for i in range(peers) if 0 <= i + by < peers]
    return lax.ppermute(x, axis, pairs)


def neutral_like(x, identity):
    return jax.tree.map(
        lambda a, e: jnp.broadcast_to(jnp.asarray(e, a.dtype), a.shape), x, identity
    )


def prefix_by_axis(x, axes, combine, identity, reverse):
    before = start = neutral_like(x, identity)
    subtotal = x
    for axis in reversed(axes):
        peers, place = (lax.axis_size(axis), lax.axis_index(axis))
        pieces = jax.tree.map(lambda part: lax.all_gather(part, axis), subtotal)
        inside, subtotal = (start, start)
        for k in reversed(range(peers)) if reverse else range(peers):
            passed = k > place if reverse else k < place
            subtotal = combine(subtotal, jax.tree.map(lambda part: part[k], pieces))
            inside = jax.tree.map(lambda new, old: jnp.where(passed, new, old), subtotal, inside)
        before = combine(inside, before)
    return before


def copy_for_each(x, axis):
    peers = lax.axis_size(axis)
    return lax.all_to_all(jnp.broadcast_to(x[None], (peers, *x.shape)), axis, 0, 0, tiled=True)


def taken_together(x, axis):
    return copy_for_each(x, axis).sum(axis=0)


def apply_each(matrices, vectors):
    return jnp.einsum("kij,kj->ki", matrices, vectors, precision=PRECISE)


def apply_transposed(matrices, vectors):
    return jnp.einsum("kji,kj->ki", matrices, vectors, precision=PRECISE)


def compose_block(loop_mats, sources):
    dimension = loop_mats.shape[-1]

    def compose_section(carried, section_item):
        product, costate = carried
        matrix, source = section_item
        return (
            (
                jnp.dot(product, matrix, precision=PRECISE),
                jnp.dot(costate, matrix, precision=PRECISE) + source,
            ),
            None,
        )

    start = (jnp.eye(dimension, dtype=jnp.float32), jnp.zeros((dimension,), jnp.float32))
    (product, costate), unused = lax.scan(
        compose_section, start, (loop_mats, sources), reverse=True
    )
    return (product, costate)


def backward_sweep(loop_mats, sources, incoming):

    def backward_section(costate, section_item):
        matrix, source = section_item
        earlier = jnp.dot(costate, matrix, precision=PRECISE) + source
        return (earlier, (costate, earlier))

    final_state, (after, before) = lax.scan(
        backward_section, incoming, (loop_mats, sources), reverse=True
    )
    return (after, before, final_state)


def forward_sweep(loop_mats, defects, pushes, entering):

    def forward_section(carried, section_item):
        matrix, defect, pushed = section_item
        correction = carried - defect
        return (jnp.dot(matrix, correction, precision=PRECISE) + pushed, correction)

    final_state, steps = lax.scan(forward_section, entering, (loop_mats, defects, pushes))
    return (steps, final_state)


def backward_join(earlier, latter):
    return (
        jnp.dot(earlier[0], latter[0], precision=PRECISE),
        jnp.dot(earlier[1], latter[0], precision=PRECISE) + latter[1],
    )


def forward_join(earlier, latter):
    return (
        jnp.dot(latter[0], earlier[0], precision=PRECISE),
        jnp.dot(latter[0], earlier[1], precision=PRECISE) + latter[1],
    )


def make_statistics(
    defect, grad_state, grad_input, slack_gap, offset, state_linear, input_linear, bound_mult
):
    return jnp.stack(
        [
            jnp.sum(defect * defect),
            jnp.sum(grad_state * grad_state) + jnp.sum(grad_input * grad_input),
            jnp.sum(slack_gap * slack_gap),
            jnp.sum(offset * offset),
            jnp.sum(state_linear * state_linear) + jnp.sum(input_linear * input_linear),
            jnp.sum(bound_mult * bound_mult),
        ]
    )


def make_norms(totals, horizon, state_count, input_count):
    primal = totals[0] / (totals[3] + floor_share * horizon * state_count)
    dual = totals[1] / (totals[4] + floor_share * horizon * (state_count + input_count))
    complement = totals[2] / (totals[5] + floor_share * horizon * input_count)
    return jnp.sqrt(jnp.stack([primal, dual, complement]))


def local(
    state_map,
    input_map,
    closed_loop,
    feedback,
    value_matrix,
    gain_inverse,
    input_weight,
    state_weight,
    state_linear,
    input_linear,
    offset,
    upper_bound,
    states,
    inputs,
    multipliers,
    bound_mult,
    active,
):
    state_count = states.shape[1]
    input_count = inputs.shape[1]
    devices = lax.axis_size(TM)
    horizon = states.shape[0] * devices
    predicted = apply_each(state_map, states) + apply_transposed(input_map, inputs)
    from_before = shifted(predicted[-1], TM, 1)
    previous = jnp.concatenate([from_before[None], predicted[:-1]], axis=0)
    defect = states - previous - offset
    from_after = shifted(multipliers[0], TM, -1)
    following = jnp.concatenate([multipliers[1:], from_after[None]], axis=0)
    grad_state = (
        state_weight * states + state_linear + multipliers - apply_transposed(state_map, following)
    )
    grad_input = (
        jnp.einsum("ij,kj->ki", input_weight, inputs, precision=PRECISE)
        + input_linear
        - apply_each(input_map, following)
        + bound_mult
    )
    slack_gap = bound_mult * (upper_bound - inputs)
    sources = apply_each(value_matrix, defect) + grad_state + apply_transposed(feedback, grad_input)
    statistics = make_statistics(
        defect, grad_state, grad_input, slack_gap, offset, state_linear, input_linear, bound_mult
    )
    product, local_costate = compose_block(closed_loop, sources)
    identity = jnp.eye(state_count, dtype=jnp.float32)
    empty_vector = jnp.zeros((state_count,), jnp.float32)
    incoming_map, incoming = prefix_by_axis(
        (product, local_costate), TM, backward_join, (identity, empty_vector), True
    )
    after, before, unused = backward_sweep(closed_loop, sources, incoming)
    pulled = apply_each(input_map, after)
    forward_gain = -apply_each(gain_inverse, grad_input + pulled)
    pushes = apply_transposed(input_map, forward_gain)
    unused_steps, local_state = forward_sweep(closed_loop, defect, pushes, empty_vector)
    entering_map, entering = prefix_by_axis(
        (product, local_state), TM, forward_join, (identity, empty_vector), False
    )
    totals = taken_together(statistics, TM)
    state_step, final_state = forward_sweep(closed_loop, defect, pushes, entering)
    chosen = active.astype(jnp.float32)
    input_step = (1.0 - chosen) * (apply_each(feedback, state_step) + forward_gain) + chosen * (
        upper_bound - inputs
    )
    multiplier_step = apply_each(value_matrix, state_step - defect) + before
    bound_step = chosen * (
        grad_input + jnp.einsum("ij,kj->ki", input_weight, input_step, precision=PRECISE) + pulled
    )
    kkt_norms = make_norms(totals, horizon, state_count, input_count)
    return (state_step, input_step, multiplier_step, bound_step, kkt_norms)


def solution(mesh):
    split = Mesh(
        mesh.devices.reshape(4, 4, 4, mesh.shape["batch"]), ("tm_0", "tm_1", "tm_2", "batch")
    )
    return jax.shard_map(
        local,
        mesh=split,
        in_specs=(
            P(BATCH_TM, None, None),
            P(BATCH_TM, None, None),
            P(BATCH_TM, None, None),
            P(BATCH_TM, None, None),
            P(BATCH_TM, None, None),
            P(BATCH_TM, None, None),
            P("batch", None),
            P(BATCH_TM, None),
            P(BATCH_TM, None),
            P(BATCH_TM, None),
            P(BATCH_TM, None),
            P(BATCH_TM, None),
            P(BATCH_TM, None),
            P(BATCH_TM, None),
            P(BATCH_TM, None),
            P(BATCH_TM, None),
            P(BATCH_TM, None),
        ),
        out_specs=(
            P(BATCH_TM, None),
            P(BATCH_TM, None),
            P(BATCH_TM, None),
            P(BATCH_TM, None),
            P("batch"),
        ),
        check_vma=False,
    )
```

profile of v0, /device:TPU:0, one launch (start us, length us, event | category | flops | bytes accessed | tf_op | source)
XLA Modules:
  0.0 349.5 jit_solution(11131336744952943273)
XLA Ops:
  7.2 5.8 %fusion.151 = f32[16,1,256]{2,1,0:T(1,128)S(1)} fusion(f32[16,256,256]{2,1,0:T(8,128)} %param.25, f32[16,256,1]{1,0,2:T(8,128)} %bitcast.322), kind=kOutput, calls=%fused_computation.171 | convolution fusion | flops 12582912 | bytes 4227072 | tf_op jit(solution)/shard_map/kij,kj->ki/dot_general | solution.py:52
  13.8 3.9 %collective-permute-start = (f32[256]{0:T(256)S(1)}, f32[256]{0:T(256)S(1)}, u32[]{:S(2)}, u32[]{:S(2)}) collective-permute-start(f32[256]{0:T(256)S(1)} %bitcast.413), channel_id=1, source_target_pairs={{0,2},{2,4},{4,6},{6,8},{8,10},{10,12},{12,14},{14,16},{16,18},{18... | collective-permute-start | bytes 3080 | tf_op jit(solution)/shard_map/ppermute | solution.py:18
  19.3 4.0 %collective-permute-done.1 = f32[256]{0:T(256)S(1)} collective-permute-done((f32[256]{0:T(256)S(1)}, f32[256]{0:T(256)S(1)}, u32[]{:S(2)}, u32[]{:S(2)}) %collective-permute-start.1) | collective-permute-done | bytes 1056 | tf_op jit(solution)/shard_map/ppermute | solution.py:18
  23.3 4.4 %fusion.155 = f32[16,1,256]{2,1,0:T(1,128)S(1)} fusion(f32[16,256,256]{2,1,0:T(8,128)} %param.25, f32[16,256,1]{1,0,2:T(8,128)S(1)} %maximum_bitcast_fusion), kind=kOutput, calls=%fused_computation.180 | convolution fusion | flops 12582912 | bytes 4227072 | tf_op jit(solution)/shard_map/kji,kj->ki/dot_general | solution.py:56
  29.3 3.5 %fusion.149 = f32[16,1,256]{2,1,0:T(1,128)S(1)} fusion(f32[16,256,256]{2,1,0:T(8,128)S(1)} %copy-done.2, f32[16,256,1]{1,0,2:T(8,128)S(1)} %bitcast.301), kind=kOutput, calls=%fused_computation.169 | convolution fusion | flops 12582912 | bytes 4227072 | tf_op jit(solution)/shard_map/kij,kj->ki/dot_general | solution.py:52
  33.7 45.5 %while.60 = (s32[]{:T(128)}, f32[256,256]{0,1:T(8,128)S(1)}, f32[256]{0:T(256)S(1)}, f32[16,256,256]{2,1,0:T(8,128)}, f32[16,256]{1,0:T(8,128)S(1)}, /*index=5*/s32[]{:T(128)}, s32[]{:T(128)}, s32[]{:T(128)}) while((s32[]{:T(128)}, f32[256,256]{0,1:T(8,128)S(1)}, f32[256]{0:T(256)S(1)}, f32[16,256,256]{2,1,0:T(8,128)}, ...), condition=%wide.region_1.0_spmd.clone, body=%wide.region_0.0_spmd.clone.sunk | while | flops 202113536 | bytes 1582199 | solution.py:74
  35.0 1.6 convolution_bitcast_fusion.2
  37.8 1.6 convolution_bitcast_fusion.2
  40.7 1.6 convolution_bitcast_fusion.2
  43.5 1.6 convolution_bitcast_fusion.2
  46.4 1.6 convolution_bitcast_fusion.2
  49.2 1.6 convolution_bitcast_fusion.2
  52.1 1.6 convolution_bitcast_fusion.2
  54.9 1.6 convolution_bitcast_fusion.2
  57.7 1.6 convolution_bitcast_fusion.2
  60.6 1.6 convolution_bitcast_fusion.2
  63.4 1.6 convolution_bitcast_fusion.2
  66.3 1.6 convolution_bitcast_fusion.2
  69.1 1.6 convolution_bitcast_fusion.2
  71.9 1.6 convolution_bitcast_fusion.2
  74.8 1.6 convolution_bitcast_fusion.2
  77.6 1.6 convolution_bitcast_fusion.2
  81.9 11.5 %all-gather.11 = f32[4,1,256]{2,1,0:T(1,128)S(1)} all-gather(f32[1,1,256]{2,1,0:T(1,128)S(1)} %bitcast.326), channel_id=7, replica_groups=mesh['tm_0'=4,'tm_1'=4,'tm_2'=4,'batch'=2] {'tm_2'}, dimensions={0}, use_global_device_ids=true | all-gather | bytes 5120 | tf_op jit(solution)/shard_map/all_gather | solution.py:32
  93.5 15.4 %all-gather.23.cloned.1.call-done = f32[1024,256]{0,1:T(8,128)} async-done(((f32[256,256]{0,1:T(8,128)}), f32[1024,256]{0,1:T(8,128)}) %all-gather.23.cloned.1.call-update) | async-done | bytes 1048592 | tf_op jit(solution)/shard_map/all_gather | solution.py:32
  114.0 9.7 %all-gather.12 = f32[4,1,256]{2,1,0:T(1,128)S(1)} all-gather(f32[1,1,256]{2,1,0:T(1,128)S(1)} %bitcast.383), channel_id=8, replica_groups=mesh['tm_0'=4,'tm_1'=4,'tm_2'=4,'batch'=2] {'tm_1'}, dimensions={0}, use_global_device_ids=true | all-gather | bytes 5120 | tf_op jit(solution)/shard_map/all_gather | solution.py:32
  125.0 1.4 fusion.113
  126.4 1.4 fusion.105
  127.7 2.1 fusion.96
  136.6 15.5 %all-gather.29.cloned.1.call-done = f32[1024,256]{1,0:T(8,128)} async-done(((f32[256,256]{1,0:T(8,128)}), f32[1024,256]{1,0:T(8,128)}) %all-gather.29.cloned.1.call-update) | async-done | bytes 1048592 | tf_op jit(solution)/shard_map/all_gather | solution.py:32
  156.9 9.7 %all-gather.13 = f32[4,1,256]{2,1,0:T(1,128)S(1)} all-gather(f32[1,1,256]{2,1,0:T(1,128)S(1)} %bitcast.384), channel_id=9, replica_groups=mesh['tm_0'=4,'tm_1'=4,'tm_2'=4,'batch'=2] {'tm_0'}, dimensions={0}, use_global_device_ids=true | all-gather | bytes 5120 | tf_op jit(solution)/shard_map/all_gather | solution.py:32
  169.9 1.3 fusion.70
  171.2 2.1 fusion.66
  173.9 4.4 %all-gather.25.cloned.1.call-done = f32[1024,256]{1,0:T(8,128)} async-done(((f32[256,256]{1,0:T(8,128)}), f32[1024,256]{1,0:T(8,128)}) %all-gather.25.cloned.1.call-update) | async-done | bytes 1048592 | tf_op jit(solution)/shard_map/all_gather | solution.py:32
  184.3 2.0 fusion.92
  186.3 2.2 fusion.36
  188.6 2.1 fusion.31
  191.6 12.7 %all-gather.31.cloned.1.call-done = f32[1024,256]{1,0:T(8,128)} async-done(((f32[256,256]{1,0:T(8,128)}), f32[1024,256]{1,0:T(8,128)}) %all-gather.31.cloned.1.call-update) | async-done | bytes 1048592 | tf_op jit(solution)/shard_map/all_gather | solution.py:32
  210.3 21.2 %while.58 = (s32[]{:T(128)}, f32[256]{0:T(256)S(1)}, f32[16,256]{1,0:T(8,128)S(1)}, f32[16,256]{1,0:T(8,128)S(1)}, f32[16,256,256]{2,1,0:T(8,128)}, /*index=5*/f...) while((s32[]{:T(128)}, f32[256]{0:T(256)S(1)}, f32[16,256]{1,0:T(8,128)S(1)}, f32[16,256]{1,0:T(8,128)S(1)}, ...), condition=%wide.region_3.0_spmd, body=%wide.region_2.0_spmd.sunk | while | flops 786691 | bytes 273529 | solution.py:87
  233.1 2.0 fusion.181
  235.7 21.1 %while.61 = (s32[]{:T(128)}, f32[256]{0:T(256)S(1)}, f32[16,256,256]{2,1,0:T(8,128)}, f32[16,256]{1,0:T(8,128)S(1)}, f32[16,256]{1,0:T(8,128)S(1)}, /*index=5*/s32[]{:T(128)}, s32[]{:T(128)}) while((s32[]{:T(128)}, f32[256]{0:T(256)S(1)}, f32[16,256,256]{2,1,0:T(8,128)}, f32[16,256]{1,0:T(8,128)S(1)}, f32[16,256]{1,0:T(8,128)S(1)}, ...), condition=%wide.region_5.0_spmd.clone, body=%wide.region_4.0_spmd.clone.sunk | while | flops 787203 | bytes 275035 | solution.py:100
  256.8 9.9 %all-gather.14 = f32[4,1,256]{2,1,0:T(1,128)S(1)} all-gather(f32[1,1,256]{2,1,0:T(1,128)S(1)} %bitcast.325), channel_id=10, replica_groups=mesh['tm_0'=4,'tm_1'=4,'tm_2'=4,'batch'=2] {'tm_2'}, dimensions={0}, use_global_device_ids=true | all-gather | bytes 5120 | tf_op jit(solution)/shard_map/all_gather | solution.py:32
  268.2 9.7 %all-gather.15 = f32[4,1,256]{2,1,0:T(1,128)S(1)} all-gather(f32[1,1,256]{2,1,0:T(1,128)S(1)} %bitcast.381), channel_id=11, replica_groups=mesh['tm_0'=4,'tm_1'=4,'tm_2'=4,'batch'=2] {'tm_1'}, dimensions={0}, use_global_device_ids=true | all-gather | bytes 5120 | tf_op jit(solution)/shard_map/all_gather | solution.py:32
  279.6 8.3 %all-gather.16 = f32[4,1,256]{2,1,0:T(1,128)S(1)} all-gather(f32[1,1,256]{2,1,0:T(1,128)S(1)} %bitcast.382), channel_id=12, replica_groups=mesh['tm_0'=4,'tm_1'=4,'tm_2'=4,'batch'=2] {'tm_0'}, dimensions={0}, use_global_device_ids=true | all-gather | bytes 5120 | tf_op jit(solution)/shard_map/all_gather | solution.py:32
  294.9 22.0 %while.59 = (s32[]{:T(128)}, f32[256]{0:T(256)S(1)}, f32[16,256]{1,0:T(8,128)S(1)}, f32[16,256,256]{2,1,0:T(8,128)}, f32[16,256]{1,0:T(8,128)S(1)}, /*index=5*/f32[16,256]{1,0:T(8,128)S(1)}, s32[]{:T(128)}, s32[]{:T(128)}) while((s32[]{:T(128)}, f32[256]{0:T(256)S(1)}, f32[16,256]{1,0:T(8,128)S(1)}, f32[16,256,256]{2,1,0:T(8,128)}, ...), condition=%wide.region_7.0_spmd, body=%wide.region_6.0_spmd.sunk | while | flops 786946 | bytes 277085 | solution.py:100
  320.5 2.5 stack.33
  323.7 4.8 %all-to-all-start = ((f32[64,1,6]{2,1,0:T(1,128)}), f32[64,1,6]{2,1,0:T(1,128)S(1)}, u32[]{:S(2)}, u32[]{:S(2)}) async-start(f32[64,1,6]{2,1,0:T(1,128)} %broadcast_in_dim.36), calls=%async_computation | async-start | bytes 65536 | tf_op jit(solution)/shard_map/all_to_all | solution.py:44
  329.3 5.7 %fusion.143 = f32[16,1,256]{2,1,0:T(1,128)S(1)} fusion(f32[16,256,256]{2,1,0:T(8,128)} %param.29, f32[16,256,1]{1,0,2:T(8,128)S(1)} %subtract_bitcast_fusion), kind=kOutput, calls=%fused_computation.162 | convolution fusion | flops 12582912 | bytes 4227072 | tf_op jit(solution)/shard_map/kij,kj->ki/dot_general | solution.py:52
  335.6 2.3 all-to-all-done
  (478 shorter events, 139.1 us)
Async XLA Ops:
  7.2 6.0 %copy-start = (f32[16,64,256]{2,1,0:T(8,128)S(1)}, f32[16,64,256]{2,1,0:T(8,128)}, u32[]{:S(2)}) copy-start(f32[16,64,256]{2,1,0:T(8,128)} %param.26) | copy-start | bytes 3145732
  7.2 6.0 %copy-start.17 = (f32[16,64]{1,0:T(8,128)S(1)}, f32[16,64]{1,0:T(8,128)}, u32[]{:S(2)}) copy-start(f32[16,64]{1,0:T(8,128)} %param.38) | copy-start | bytes 12292
  7.2 10.6 %copy-start.18 = (f32[16,256]{1,0:T(8,128)S(1)}, f32[16,256]{1,0:T(8,128)}, u32[]{:S(2)}) copy-start(f32[16,256]{1,0:T(8,128)} %param.39) | copy-start | bytes 49156
  7.2 101.6 %all-gather.23.cloned.1.call-start = ((), (), s32[]{:S(2)}) async-start(), calls=%async_computation.1 | async-start | bytes 1310720 | tf_op jit(solution)/shard_map/all_gather | solution.py:32
  13.1 15.6 %copy-start.19 = (f32[16,256]{1,0:T(8,128)S(1)}, f32[16,256]{1,0:T(8,128)}, u32[]{:S(2)}) copy-start(f32[16,256]{1,0:T(8,128)} %param.37) | copy-start | bytes 49156
  13.1 15.6 %copy-start.24 = (f32[16,256]{1,0:T(8,128)S(1)}, f32[16,256]{1,0:T(8,128)}, u32[]{:S(2)}) copy-start(f32[16,256]{1,0:T(8,128)} %param.33) | copy-start | bytes 49156
  13.1 15.6 %copy-start.25 = (f32[16,256]{1,0:T(8,128)S(1)}, f32[16,256]{1,0:T(8,128)}, u32[]{:S(2)}) copy-start(f32[16,256]{1,0:T(8,128)} %param.32) | copy-start | bytes 49156
  13.1 15.6 %copy-start.26 = (f32[16,256]{1,0:T(8,128)S(1)}, f32[16,256]{1,0:T(8,128)}, u32[]{:S(2)}) copy-start(f32[16,256]{1,0:T(8,128)} %param.35) | copy-start | bytes 49156
  13.8 14.8 %collective-permute-start = (f32[256]{0:T(256)S(1)}, f32[256]{0:T(256)S(1)}, u32[]{:S(2)}, u32[]{:S(2)}) collective-permute-start(f32[256]{0:T(256)S(1)} %bitcast.413), channel_id=1, source_target_pairs={{0,2},{2,4},{4,6},{6,8},{8,10},{10,12},{12,14},{14,16},{16,18},{18... | collective-permute-start | bytes 3080 | tf_op jit(solution)/shard_map/ppermute | solution.py:18
  17.8 5.5 %collective-permute-start.1 = (f32[256]{0:T(256)S(1)}, f32[256]{0:T(256)S(1)}, u32[]{:S(2)}, u32[]{:S(2)}) collective-permute-start(f32[256]{0:T(256)S(1)} %bitcast.414), channel_id=1, source_target_pairs={{2,0},{4,2},{6,4},{8,6},{10,8},{12,10},{14,12},{16,14},{18,16},{20... | collective-permute-start | bytes 3080 | tf_op jit(solution)/shard_map/ppermute | solution.py:18
  19.3 10.0 %copy-start.2 = (f32[16,256,256]{2,1,0:T(8,128)S(1)}, f32[16,256,256]{2,1,0:T(8,128)}, u32[]{:S(2)}) copy-start(f32[16,256,256]{2,1,0:T(8,128)} %param.29) | copy-start | bytes 12582916
  23.3 9.6 %copy-start.16 = (f32[64,64]{1,0:T(8,128)S(1)}, f32[64,64]{1,0:T(8,128)}, u32[]{:S(2)}) copy-start(f32[64,64]{1,0:T(8,128)} %param.31) | copy-start | bytes 49156
  23.3 9.6 %copy-start.20 = (f32[16,64]{1,0:T(8,128)S(1)}, f32[16,64]{1,0:T(8,128)}, u32[]{:S(2)}) copy-start(f32[16,64]{1,0:T(8,128)} %param.40) | copy-start | bytes 12292
  23.3 9.6 %copy-start.23 = (f32[16,64]{1,0:T(8,128)S(1)}, f32[16,64]{1,0:T(8,128)}, u32[]{:S(2)}) copy-start(f32[16,64]{1,0:T(8,128)} %param.34) | copy-start | bytes 12292
  23.3 9.8 %copy-start.5 = (f32[16,64,256]{2,1,0:T(8,128)S(1)}, f32[16,64,256]{2,1,0:T(8,128)}, u32[]{:S(2)}) copy-start(f32[16,64,256]{2,1,0:T(8,128)} %param.28) | copy-start | bytes 3145732
  79.2 0.7 copy-start.3
  79.9 72.2 %all-gather.29.cloned.1.call-start = ((), (), s32[]{:S(2)}) async-start(), calls=%async_computation.4 | async-start | bytes 1310720 | tf_op jit(solution)/shard_map/all_gather | solution.py:32
  108.8 21.2 %copy-start.1 = (f32[1024,256]{0,1:T(8,128)S(1)}, f32[1024,256]{0,1:T(8,128)}, u32[]{:S(2)}) copy-start(f32[1024,256]{0,1:T(8,128)} %all-gather.23.cloned.1.call-done) | copy-start | bytes 3145732
  129.8 48.4 %all-gather.25.cloned.1.call-start = ((), (), s32[]{:S(2)}) async-start(), calls=%async_computation.2 | async-start | bytes 1310720 | tf_op jit(solution)/shard_map/all_gather | solution.py:32
  130.5 0.7 copy-start.7
  134.7 39.0 %copy-start.12 = (f32[256,256]{1,0:T(8,128)S(1)}, f32[256,256]{1,0:T(8,128)}, u32[]{:S(2)}) copy-start(f32[256,256]{1,0:T(8,128)} %fusion.41) | copy-start | bytes 786436
  134.7 69.6 %all-gather.31.cloned.1.call-start = ((), (), s32[]{:S(2)}) async-start(), calls=%async_computation.5 | async-start | bytes 1310720 | tf_op jit(solution)/shard_map/all_gather | solution.py:32
  167.8 0.7 copy-start.13
  171.2 2.7 copy-start.8
  173.4 115.1 %all-gather.27.cloned.1.call-start = ((), (), s32[]{:S(2)}) async-start(), calls=%async_computation.3 | async-start | bytes 1310720 | tf_op jit(solution)/shard_map/all_gather | solution.py:32
  178.3 12.5 %copy-start.4 = (f32[1024,256]{1,0:T(8,128)S(1)}, f32[1024,256]{1,0:T(8,128)}, u32[]{:S(2)}) copy-start(f32[1024,256]{1,0:T(8,128)} %all-gather.25.cloned.1.call-done) | copy-start | bytes 3145732
  179.6 0.7 copy-start.14
  181.6 0.7 copy-start.9
  183.6 0.7 copy-start.10
  207.8 80.3 %copy-start.11 = (f32[256,256]{1,0:T(8,128)S(1)}, f32[256,256]{1,0:T(8,128)}, u32[]{:S(2)}) copy-start(f32[256,256]{1,0:T(8,128)} %fusion.26) | copy-start | bytes 786436
  235.0 84.2 %copy-start.21 = (s32[16,64]{1,0:T(8,128)S(1)}, s32[16,64]{1,0:T(8,128)}, u32[]{:S(2)}) copy-start(s32[16,64]{1,0:T(8,128)} %param.41) | copy-start | bytes 12292
  268.1 48.9 %copy-start.6 = (f32[16,64,256]{2,1,0:T(8,128)S(1)}, f32[16,64,256]{2,1,0:T(8,128)}, u32[]{:S(2)}) copy-start(f32[16,64,256]{2,1,0:T(8,128)} %param.28) | copy-start | bytes 3145732
  317.0 25.9 %copy-start.15 = (f32[16,256]{1,0:T(8,128)}, f32[16,256]{1,0:T(8,128)S(1)}, u32[]{:S(2)}) copy-start(f32[16,256]{1,0:T(8,128)S(1)} %get-tuple-element.286) | copy-start | bytes 49156
  320.5 22.4 %copy-start.22 = (f32[16,64]{1,0:T(8,128)}, f32[16,64]{1,0:T(8,128)S(1)}, u32[]{:S(2)}) copy-start(f32[16,64]{1,0:T(8,128)S(1)} %get-tuple-element.424) | copy-start | bytes 12292
  323.7 14.1 %all-to-all-start = ((f32[64,1,6]{2,1,0:T(1,128)}), f32[64,1,6]{2,1,0:T(1,128)S(1)}, u32[]{:S(2)}, u32[]{:S(2)}) async-start(f32[64,1,6]{2,1,0:T(1,128)} %broadcast_in_dim.36), calls=%async_computation | async-start | bytes 65536 | tf_op jit(solution)/shard_map/all_to_all | solution.py:44
Sparse Core Ops, SparseCore 0:
  80.0 28.7 all-gather.22
  129.9 22.1 all-gather.28
  153.8 24.4 all-gather.24
  179.8 24.4 all-gather.30
  205.8 24.4 all-gather.26
where the time goes:
time: 353 us; the launch traced here: 349 us
  matrix products  182 us (52%)
  blocking collectives  58.9 us (17%)
  waiting for transfers between devices  54.2 us (15%)
  between operations  21.1 us (6%)
  local copies, waits for them, and re-layouts  11.8 us (3%)
  starting transfers between devices  10.5 us (3%)
  other arithmetic  6.9 us (2%)
  loops' own time  4.16 us (1%)
    all_gather x6, blocking collectives, prefix_by_axis(): pieces = jax.tree.map(lambda part: lax.all_gather(part, axis), subtotal)  58.9 us
    all_gather x5, waiting for transfers between devices, prefix_by_axis(): pieces = jax.tree.map(lambda part: lax.all_gather(part, axis), subtotal)  47.9 us
    dot_general x32, matrix products, forward_section(): return (jnp.dot(matrix, correction, precision=PRECISE) + pushed, correction)  39.2 us
    dot_general x16, matrix products, compose_section(): jnp.dot(product, matrix, precision=PRECISE)  24.8 us
    dot_general x7, matrix products, apply_each(): return jnp.einsum('kij,kj->ki', matrices, vectors, precision=PRECISE)  19.9 us
    dot_general x16, matrix products, backward_section(): earlier = jnp.dot(costate, matrix, precision=PRECISE) + source  18.8 us
    dot_general x16, matrix products, compose_section(): jnp.dot(costate, matrix, precision=PRECISE) + source  18.7 us
    dot_general x15, matrix products, backward_join(): jnp.dot(earlier[1], latter[0], precision=PRECISE) + latter[1]  15.9 us
  transfers between devices with their start and end apart: 8, of which 6 were waited for; matrix products, arithmetic and copies ran while one was open for 27% of the time, Pallas kernels for 0%

commit v1 on v0

v1 whole, which is shorter than its diff:
```python
import functools

import jax
import jax.numpy as jnp
from jax import lax
from jax.experimental import pallas as pl
from jax.experimental.pallas import tpu as pltpu
from jax.sharding import Mesh
from jax.sharding import PartitionSpec as P

TM = ("tm_0", "tm_1", "tm_2")
BATCH_TM = ("batch", "tm_0", "tm_1", "tm_2")
F32 = jnp.float32
BF16 = jnp.bfloat16
floor_share = 0.001
VMEM = pltpu.VMEM
SMEM = pltpu.SMEM


def halves(x):
    high = x.astype(BF16)
    low = (x - high.astype(F32)).astype(BF16)
    return high, low


def dot(a, b, ca, cb):
    return lax.dot_general(a, b, (((ca,), (cb,)), ((), ())), preferred_element_type=F32)


def mat_mul(a, b, ca=1, cb=0):
    ah, al = halves(a)
    bh, bl = halves(b)
    return dot(ah, bh, ca, cb) + (dot(ah, bl, ca, cb) + dot(al, bh, ca, cb))


def row_halves(v):
    high = v.astype(BF16).astype(F32)
    row = lax.broadcasted_iota(jnp.int32, (8, v.shape[1]), 0)
    both = jnp.where(row == 0, high, jnp.where(row == 1, v - high, 0.0))
    return both.astype(BF16)


def vec_mat(v, m, cb=0):
    lhs = row_halves(v)
    mh, ml = halves(m)
    r = dot(lhs, mh, 1, cb) + dot(lhs, ml, 1, cb)
    return jnp.sum(r, axis=0, keepdims=True)


def last_prediction_body(ready, f_ref, m_ref, x_ref, u_ref, out_ref):
    ready(0)
    v = vec_mat(x_ref[7:8, :], f_ref[0], 1) + vec_mat(u_ref[7:8, :], m_ref[0])
    out_ref[...] = jnp.broadcast_to(v, (8, 256))


def block_product_body(ready, a_ref, p_ref, pair_ref, quad_ref, half_ref):
    for j in range(4):
        ready(j)
        low = mat_mul(a_ref[4 * j + 1], a_ref[4 * j])
        high = mat_mul(a_ref[4 * j + 3], a_ref[4 * j + 2])
        pair_ref[j] = high
        quad_ref[j] = mat_mul(high, low)
        if j == 1:
            half_ref[...] = mat_mul(quad_ref[1], quad_ref[0])
    p_ref[...] = mat_mul(mat_mul(quad_ref[3], quad_ref[2]), half_ref[...])


def total(x):
    return jnp.sum(jnp.sum(x, axis=0, keepdims=True), axis=1, keepdims=True)


def sources_body(
    ready, f_ref, m_ref, v_ref, k_ref, a_ref,
    x_ref, u_ref, mult_ref, bm_ref, ub_ref, off_ref, sw_ref, sl_ref, il_ref, iw_ref,
    quad_ref, half_ref, before_ref, next_ref,
    defect_ref, gi_ref, src_ref, b_ref, c_ref, stat_ref,
    gs_ref,
):
    gi_ref[...] = mat_mul(u_ref[...], iw_ref[...], 1, 1) + il_ref[...] + bm_ref[...]
    gs_ref[...] = sw_ref[...] * x_ref[...] + sl_ref[...] + mult_ref[...]
    src_ref[...] = x_ref[...] - off_ref[...]
    prev = before_ref[0:1, :]
    for i in range(4):
        ready(i)
        for j in range(4):
            k = i * 4 + j
            follow = next_ref[0:1, :] if k == 15 else mult_ref[k + 1:k + 2, :]
            gs = gs_ref[k:k + 1, :] - vec_mat(follow, f_ref[k])
            gs_ref[k:k + 1, :] = gs
            gi = gi_ref[k:k + 1, :] - vec_mat(follow, m_ref[k], 1)
            gi_ref[k:k + 1, :] = gi
            d = src_ref[k:k + 1, :] - prev
            defect_ref[k:k + 1, :] = d
            src_ref[k:k + 1, :] = vec_mat(d, v_ref[k]) + gs + vec_mat(gi, k_ref[k])
            if k < 15:
                prev = vec_mat(x_ref[k:k + 1, :], f_ref[k], 1) + vec_mat(u_ref[k:k + 1, :], m_ref[k])
    b = [src_ref[4 * j + 3:4 * j + 4, :] for j in range(4)]
    for j in range(4):
        b_ref[4 * j + 3:4 * j + 4, :] = b[j]
    for m in (2, 1, 0):
        for j in range(4):
            k = 4 * j + m
            b[j] = vec_mat(b[j], a_ref[k]) + src_ref[k:k + 1, :]
            b_ref[k:k + 1, :] = b[j]
    upper = b[2] + vec_mat(b[3], quad_ref[2])
    c = b[0] + vec_mat(b[1], quad_ref[0]) + vec_mat(upper, half_ref[...])
    c_ref[...] = jnp.broadcast_to(c, (8, 256))

    gap = bm_ref[...] * (ub_ref[...] - u_ref[...])
    d, gs, gi = defect_ref[...], gs_ref[...], gi_ref[...]
    off, sl, il, bm = off_ref[...], sl_ref[...], il_ref[...], bm_ref[...]
    found = (
        total(d * d),
        total(gs * gs) + total(gi * gi),
        total(gap * gap),
        total(off * off),
        total(sl * sl) + total(il * il),
        total(bm * bm),
    )
    lane = lax.broadcasted_iota(jnp.int32, (8, 128), 1)
    out = jnp.zeros((8, 128), F32)
    for n, s in enumerate(found):
        out = jnp.where(lane == n, s, out)
    stat_ref[...] = out


def weight_body(ready, a_ref, m_ref, g_ref, pair_ref, quad_ref, half_ref, w_ref, third_ref, b_ref, gb_ref):
    third_ref[...] = mat_mul(quad_ref[2], half_ref[...])
    ready(0)
    for j in range(4):
        k = 4 * j
        r = 256 * j
        b_ref[r:r + 64, :] = mat_mul(m_ref[k], a_ref[k + 1], 1, 1)
        b_ref[r + 64:r + 128, :] = m_ref[k + 1]
        b_ref[r + 128:r + 192, :] = mat_mul(m_ref[k + 2], a_ref[k + 3], 1, 1)
        b_ref[r + 192:r + 256, :] = m_ref[k + 3]
        b_ref[r:r + 128, :] = mat_mul(b_ref[r:r + 128, :], pair_ref[j], 1, 1)
    for j in (1, 2, 3):
        b_ref[0:256 * j, :] = mat_mul(b_ref[0:256 * j, :], quad_ref[j], 1, 1)
    for k in range(16):
        gb_ref[64 * k:64 * k + 64, :] = mat_mul(g_ref[k], b_ref[64 * k:64 * k + 64, :])
    w_ref[...] = mat_mul(b_ref[...], gb_ref[...], 0, 0)


def sweep_body(
    ready, a_ref, m_ref, g_ref, *refs,
):
    quad_ref, b_ref, src_ref, gi_ref, defect_ref = refs[:5]
    lam_ref = refs[5] if len(refs) > 12 else None
    before_ref, gain_ref, base_ref, push_ref, entry_ref, end_ref, after_ref = refs[-7:]
    lams = [None, None, None, jnp.zeros((1, 256), F32) if lam_ref is None else lam_ref[0:1, :]]
    for j in (2, 1, 0):
        lams[j] = vec_mat(lams[j + 1], quad_ref[j + 1]) + b_ref[4 * j + 4:4 * j + 5, :]
    before_ref[0:1, :] = vec_mat(lams[0], quad_ref[0]) + b_ref[0:1, :]
    for j in range(3):
        before_ref[4 * j + 4:4 * j + 5, :] = lams[j]
    ready(0)
    for m in (3, 2, 1, 0):
        for j in range(4):
            k = 4 * j + m
            after_ref[k:k + 1, :] = lams[j]
            if m > 0:
                lams[j] = vec_mat(lams[j], a_ref[k]) + src_ref[k:k + 1, :]
                before_ref[k:k + 1, :] = lams[j]
    for k in range(16):
        base = gi_ref[k:k + 1, :] + vec_mat(after_ref[k:k + 1, :], m_ref[k], 1)
        base_ref[k:k + 1, :] = base
        gain = -vec_mat(base, g_ref[k])
        gain_ref[k:k + 1, :] = gain
        push_ref[k:k + 1, :] = vec_mat(gain, m_ref[k])
    ends = [jnp.zeros((1, 256), F32)] * 4
    for m in range(4):
        for j in range(4):
            k = 4 * j + m
            step = ends[j] - defect_ref[k:k + 1, :]
            ends[j] = vec_mat(step, a_ref[k], 1) + push_ref[k:k + 1, :]
    entry_ref[...] = jnp.zeros_like(entry_ref)
    e = ends[0]
    for j in (1, 2, 3):
        entry_ref[j:j + 1, :] = e
        e = vec_mat(e, quad_ref[j], 1) + ends[j]
    end_ref[...] = jnp.broadcast_to(e, (8, 256))


def order(ref, place, own, minus, plus, across):
    ref[place] = own
    ref[lax.rem(place + 1, 4)] = plus
    ref[lax.rem(place + 2, 4)] = across
    ref[lax.rem(place + 3, 4)] = minus


def join_body(ready, idx_ref, *refs, axis):
    place = idx_ref[axis]
    maps_ref, vectors_ref, out_ref = refs[-3:]
    parts = refs[:4]
    order(maps_ref, place, *[r[0:256, :] for r in parts])
    order(vectors_ref, place, *([r[...] for r in refs[4:8]] if len(refs) > 7 else [r[256:264, :] for r in parts]))
    high = mat_mul(maps_ref[3], maps_ref[2])
    low = mat_mul(maps_ref[1], maps_ref[0])
    v = vectors_ref[3, 0:1, :]
    for j in (2, 1, 0):
        v = vec_mat(v, maps_ref[j]) + vectors_ref[j, 0:1, :]
    out_ref[0:256, :] = mat_mul(high, low)
    out_ref[256:264, :] = jnp.broadcast_to(v, (8, 256))


def chain_back(lam, maps, order, place):
    picked = lam
    for j in (3, 2, 1):
        lam = vec_mat(lam, maps[j]) + order[j, 0:1, :]
        picked = jnp.where(place == j - 1, lam, picked)
    return picked


def costate_body(
    ready, idx_ref, h0_ref, hm_ref, hp_ref, h2_ref,
    gx_ref, cx_ref, pz_ref, cz_ref, w_ref, s0_ref, stat_ref,
    lam_ref, msg_ref, hy_ref, order_ref,
):
    y = idx_ref[0]
    x = idx_ref[1]
    z = idx_ref[2]
    refs = (h0_ref, hm_ref, hp_ref, h2_ref)
    order(hy_ref, y, *[r[0:256, :] for r in refs])
    order(order_ref, y, *[r[256:264, :] for r in refs])
    lam = chain_back(jnp.zeros((1, 256), F32), hy_ref, order_ref, y)
    lam = chain_back(lam, gx_ref, cx_ref, x)
    lam = chain_back(lam, pz_ref, cz_ref, z)
    lam_ref[...] = jnp.broadcast_to(lam, (8, 256))
    s = s0_ref[0:1, :] - vec_mat(lam, w_ref[...])
    u1 = s
    for j in (1, 2, 3):
        s = jnp.where(z + j <= 3, vec_mat(s, pz_ref[jnp.minimum(z + j, 3)], 1), s)
    u2 = s
    for j in (1, 2, 3):
        s = jnp.where(x + j <= 3, vec_mat(s, gx_ref[jnp.minimum(x + j, 3)], 1), s)
    u3 = s
    d = lax.broadcasted_iota(jnp.int32, (64, 256), 0)
    group = lax.shift_right_logical(d, 2)
    plane = lax.shift_right_logical(d, 4)
    msg_ref[:, 0, 0:256] = jnp.where(group == y * 4 + x, u1, jnp.where(plane == y, u2, u3))
    msg_ref[:, 0, 256:384] = jnp.broadcast_to(stat_ref[0:1, :], (64, 128))


def chain_forth(e, maps, sums, place):
    picked = e
    for j in (0, 1, 2):
        e = vec_mat(e, maps[j], 1) + sums[j]
        picked = jnp.where(place == j + 1, e, picked)
    return picked


def finish_body(
    ready, idx_ref, a_ref, v_ref, k_ref, active_ref, ub_ref, u_ref, iw_ref,
    h0_ref, hm_ref, hp_ref, h2_ref, gx_ref, pz_ref, quad_ref, half_ref, third_ref,
    entry_ref, push_ref, defect_ref, before_ref, gain_ref, base_ref, msg_ref,
    ss_ref, is_ref, ms_ref, bs_ref, norm_ref, hy_ref,
    *, horizon,
):
    order(hy_ref, idx_ref[0], *[r[0:256, :] for r in (h0_ref, hm_ref, hp_ref, h2_ref)])
    y = idx_ref[0]
    x = idx_ref[1]
    z = idx_ref[2]
    d = lax.broadcasted_iota(jnp.int32, (64, 256), 0)
    plane = lax.shift_right_logical(d, 4)
    group = lax.shift_right_logical(d, 2)
    msg = msg_ref[:, 0, 0:256]

    def picked(mask):
        return jnp.sum(jnp.where(mask, msg, 0.0), axis=0, keepdims=True)

    e = chain_forth(jnp.zeros((1, 256), F32), hy_ref, [picked(plane == j) for j in range(3)], y)
    e = chain_forth(e, gx_ref, [picked(group == y * 4 + j) for j in range(3)], x)
    e = chain_forth(e, pz_ref, [picked(d == y * 16 + x * 4 + j) for j in range(3)], z)
    sums = jnp.sum(msg_ref[:, 0, 256:384], axis=0, keepdims=True)
    lane = lax.broadcasted_iota(jnp.int32, (1, 128), 1)
    share = floor_share * horizon
    floors = jnp.where(lane == 0, share * 256, jnp.where(lane == 1, share * 320, share * 64))
    norm_ref[...] = jnp.sqrt(sums / (pltpu.roll(sums, 125, 1) + floors))[:, 0:3]
    ends = [
        e,
        vec_mat(e, quad_ref[0], 1) + entry_ref[1:2, :],
        vec_mat(e, half_ref[...], 1) + entry_ref[2:3, :],
        vec_mat(e, third_ref[...], 1) + entry_ref[3:4, :],
    ]
    ready(0)
    for m in range(4):
        for j in range(4):
            k = 4 * j + m
            step = ends[j] - defect_ref[k:k + 1, :]
            ss_ref[k:k + 1, :] = step
            if m < 3:
                ends[j] = vec_mat(step, a_ref[k], 1) + push_ref[k:k + 1, :]
    for k in range(16):
        step = ss_ref[k:k + 1, :]
        ms_ref[k:k + 1, :] = vec_mat(step - defect_ref[k:k + 1, :], v_ref[k]) + before_ref[k:k + 1, :]
        is_ref[k:k + 1, :] = vec_mat(step, k_ref[k], 1) + gain_ref[k:k + 1, :]
    chosen = active_ref[...].astype(F32)
    step = (1.0 - chosen) * is_ref[...] + chosen * (ub_ref[...] - u_ref[...])
    is_ref[...] = step
    bs_ref[...] = chosen * (base_ref[...] + mat_mul(step, iw_ref[...], 1, 1))


def sds(*shape):
    return jax.ShapeDtypeStruct(shape, F32)


SCALARS = pl.BlockSpec(memory_space=SMEM)
FULL = pl.BlockSpec(memory_space=VMEM)


def in_vmem(shape):
    return pltpu.VMEM(shape, F32)


def call(body, scalars, big, small, near, outs, scratch, chunks=1, final=False, away=()):
    ns, nb, nm, nn, no = len(scalars), len(big), len(small), len(near), len(outs)
    far = [b if isinstance(b, tuple) else (b, 0, b.shape[0]) for b in list(big) + list(small)]

    def kernel(*refs):
        refs = list(refs)

        def take(n):
            out = refs[:n]
            del refs[:n]
            return out

        scalar_refs, far_refs, near_refs, out_refs, local_refs = take(ns), take(nb + nm), take(nn), take(no), take(nb + nm)
        sems = refs.pop() if far else None
        moves = [[] for _ in range(chunks)]
        first = []
        n = 0
        for at, ((_, low, size), src, dst) in enumerate(zip(far, far_refs, local_refs)):
            pieces = chunks if at < nb else 1
            step = size // pieces
            for c in range(pieces):
                move = pltpu.make_async_copy(
                    src.at[pl.ds(low + c * step, step)], dst.at[pl.ds(c * step, step)], sems.at[n]
                )
                (moves[c] if at < nb else first).append(move)
                n += 1
        for move in first:
            move.start()
        for group in moves:
            for move in group:
                move.start()
        for move in first:
            move.wait()

        def ready(c):
            for move in moves[c]:
                move.wait()

        body(ready, *scalar_refs, *local_refs, *near_refs, *out_refs, *refs)

    rooms = [pltpu.VMEM((size,) + a.shape[1:], a.dtype) for a, _, size in far]
    count = nb * chunks + nm
    sems = [pltpu.SemaphoreType.DMA((count,))] if far else []
    return pl.pallas_call(
        kernel,
        in_specs=[SCALARS] * ns + [pl.BlockSpec(memory_space=pltpu.HBM)] * (nb + nm) + [FULL] * nn,
        out_specs=[FULL] * no,
        out_shape=[sds(*o) if final else (pltpu.HBM(o, F32) if n in away else in_vmem(o)) for n, o in enumerate(outs)],
        scratch_shapes=rooms + scratch + sems,
        compiler_params=pltpu.CompilerParams(vmem_limit_bytes=24 * 1024 * 1024),
    )(*scalars, *[pltpu.with_memory_space_constraint(a, pltpu.HBM) for a, _, _ in far], *near)


def room(*shape):
    return VMEM(shape, F32)


def turned(x, axis):
    def move(by):
        return lax.ppermute(x, axis, [(i, (i + by) % 4) for i in range(4)])

    return move(1), move(-1), move(2)


def shifted(x, by):
    pairs = [(i, i + by) for i in range(64) if 0 <= i + by < 64]
    return lax.ppermute(x, TM, pairs)


def local(
    state_map,
    input_map,
    closed_loop,
    feedback,
    value_matrix,
    gain_inverse,
    input_weight,
    state_weight,
    state_linear,
    input_linear,
    offset,
    upper_bound,
    states,
    inputs,
    multipliers,
    bound_mult,
    active,
):
    place = jnp.stack([lax.axis_index(a) for a in TM]).astype(jnp.int32)

    place, ahead = lax.optimization_barrier((place, multipliers[:8]))
    from_after = shifted(ahead, -1)
    (last,) = call(
        last_prediction_body, [],
        [(state_map, 15, 1), (input_map, 15, 1), (states, 8, 8), (inputs, 8, 8)], [], [],
        [(8, 256)], [],
    )
    from_before = shifted(last, 1)

    loops, last = lax.optimization_barrier((closed_loop, last))
    product, pairs, quads, half = call(
        block_product_body, [], [loops], [], [],
        [(256, 256), (4, 256, 256), (4, 256, 256), (256, 256)], [], chunks=4,
    )
    near = turned(product, "tm_2")

    defect, grad_input, sources, inner, costate, statistics = call(
        sources_body, [],
        [state_map, input_map, value_matrix, feedback, closed_loop],
        [states, inputs, multipliers, bound_mult, upper_bound, offset, state_weight, state_linear, input_linear, input_weight],
        [quads, half, from_before, from_after],
        [(16, 256), (16, 64), (16, 256), (16, 256), (8, 256), (8, 128)],
        [room(16, 256)], chunks=4,
    )
    costates = turned(costate, "tm_2")

    def join(axis, *parts):
        return call(
            functools.partial(join_body, axis=axis), [place], [], [],
            list(parts),
            [(4, 256, 256), (4, 8, 256), (264, 256)], [],
        )

    maps_z, vectors_z, group = join(2, product, *near, costate, *costates)
    near_x = turned(group, "tm_1")

    loops, group = lax.optimization_barrier((closed_loop, group))
    weight, third = call(
        weight_body, [], [loops, input_map, gain_inverse], [], [pairs, quads, half],
        [(256, 256), (256, 256)], [room(1024, 256), room(1024, 256)],
    )
    near_x, weight, third = lax.optimization_barrier((near_x, weight, third))

    maps_x, vectors_x, plane = join(1, group, *near_x)
    near_y = turned(plane, "tm_0")

    def sweep(loops, far, near, away):
        return call(
            sweep_body, [], [loops, input_map, gain_inverse], far, near,
            [(16, 256), (16, 64), (16, 64), (16, 256), (8, 256), (8, 256)], [room(16, 256)], away=away,
        )

    local_parts = [quads, inner, sources, grad_input, defect]
    loops, plane = lax.optimization_barrier((closed_loop, plane))
    local_state = sweep(loops, [], local_parts, range(5))[5]

    incoming, message = call(
        costate_body, [place], [], [],
        [plane, *near_y, maps_x, vectors_x, maps_z, vectors_z, weight, local_state, statistics],
        [(8, 256), (64, 1, 384)], [room(4, 256, 256), room(4, 8, 256)], away=(0, 1),
    )

    received = lax.all_to_all(message, TM, 0, 0, tiled=True)

    before, gain, base, push, entry, _ = sweep(
        closed_loop, local_parts + [incoming], [], range(6)
    )

    state_step, input_step, multiplier_step, bound_step, sums = call(
        functools.partial(finish_body, horizon=states.shape[0] * lax.axis_size(TM)), [place],
        [closed_loop, value_matrix, feedback],
        [active, upper_bound, inputs, input_weight, plane, *near_y, maps_x, maps_z, quads, half, third]
        + [entry, push, defect, before, gain, base],
        [received],
        [(16, 256), (16, 64), (16, 256), (16, 64), (1, 3)], [room(4, 256, 256)], final=True,
    )

    kkt_norms = sums.reshape(3)
    return (state_step, input_step, multiplier_step, bound_step, kkt_norms)


def solution(mesh):
    split = Mesh(
        mesh.devices.reshape(4, 4, 4, mesh.shape["batch"]), ("tm_0", "tm_1", "tm_2", "batch")
    )

    return jax.shard_map(
        local,
        mesh=split,
        in_specs=(P(BATCH_TM, None, None),) * 6 + (P("batch", None),) + (P(BATCH_TM, None),) * 10,
        out_specs=(P(BATCH_TM, None),) * 4 + (P("batch"),),
        check_vma=False,
    )
```

time: 353 us -> 111 us (0.31)
  matrix products: 182 us -> 0 us
  blocking collectives: 58.9 us -> 0 us
  Pallas kernels: 0 us -> 53.1 us
  waiting for transfers between devices: 54.2 us -> 11.9 us
  starting transfers between devices: 10.5 us -> 36.3 us
  between operations: 21.1 us -> 1.06 us
  other arithmetic: 6.9 us -> 0.08 us
  loops' own time: 4.16 us -> 0 us
    dot_general x143 -> x0, matrix products: 182 us -> none  [the longest x32 39.2 us: forward_section(): return (jnp.dot(matrix, correction, precision=PRECISE) + pushed, correction)]
    all_gather x6 -> x0, blocking collectives: 58.9 us -> none  [prefix_by_axis(): pieces = jax.tree.map(lambda part: lax.all_gather(part, axis), subtotal)]
    pallas_call x0 -> x10, Pallas kernels: none -> 53.1 us  [call(): pl.pallas_call(kernel, in_specs=[SCALARS] * ns + [pl.BlockSpec(memory_spa...]
    all_gather x5 -> x0, waiting for transfers between devices: 47.9 us -> none  [prefix_by_axis(): pieces = jax.tree.map(lambda part: lax.all_gather(part, axis), subtotal)]
    ppermute x2 -> x14, starting transfers between devices: 5.23 us -> 30.7 us  [the longest x12 24.8 us: move(): return lax.ppermute(x, axis, [(i, (i + by) % 4) for i in range(4)])]
    ppermute x2 -> x14, waiting for transfers between devices: 3.97 us -> 10.7 us  [the longest x12 5.8 us: move(): return lax.ppermute(x, axis, [(i, (i + by) % 4) for i in range(4)])]
    another operation x4 -> x0, loops' own time: 4.16 us -> none  [the longest x2 2.56 us: forward_sweep(): lax.scan(forward_section, entering, (loop_mats, defects, pushes))]
    unnamed x55 -> x44, local copies, waits for them, and re-layouts: 4.43 us -> 8.38 us
  transfers between devices with their start and end apart: 8 -> 15, of which waited for: 6 -> 6; matrix products, arithmetic and copies ran while one was open for 27% -> 0% of each run, Pallas kernels for 0% -> 28%
where the time goes in v1:
time: 111 us
  Pallas kernels  53.1 us (48%)
  starting transfers between devices  36.3 us (33%)
  waiting for transfers between devices  11.9 us (11%)
  local copies, waits for them, and re-layouts  8.38 us (8%)
    pallas_call x10, Pallas kernels, call(): pl.pallas_call(kernel, in_specs=[SCALARS] * ns + [pl.BlockSpec(memory_spa...  53.1 us
    ppermute x12, starting transfers between devices, move(): return lax.ppermute(x, axis, [(i, (i + by) % 4) for i in range(4)])  24.8 us
    unnamed x44, local copies, waits for them, and re-layouts  8.38 us
    ppermute x2, starting transfers between devices, shifted(): return lax.ppermute(x, TM, pairs)  5.83 us
    ppermute x12, waiting for transfers between devices, move(): return lax.ppermute(x, axis, [(i, (i + by) % 4) for i in range(4)])  5.8 us
    all_to_all x1, starting transfers between devices, local(): received = lax.all_to_all(message, TM, 0, 0, tiled=True)  5.64 us
    ppermute x2, waiting for transfers between devices, shifted(): return lax.ppermute(x, TM, pairs)  4.92 us
  transfers between devices with their start and end apart: 15, of which 6 were waited for; matrix products, arithmetic and copies ran while one was open for 0% of the time, Pallas kernels for 28%

profile of v1, /device:TPU:0, one launch (start us, length us, event | category | flops | bytes accessed | tf_op | source)
XLA Modules:
  0.0 110.8 jit_solution(31600798806261615)
XLA Ops:
  0.6 0.0 copy-start.21
  0.6 1.2 %shard_map.200 = f32[8,256]{1,0:T(8,128)S(1)} custom-call(f32[16,256,256]{2,1,0:T(8,128)} %refs_0_.5, f32[16,64,256]{2,1,0:T(8,128)} %refs_1_.10, f32[16,256]{1,0:T(8,128)} %refs_5_.2, f32[16,64]{1,0:T(8,128)} %refs_6_.3), custom_call_target="tpu_custom_call" | custom-call | tf_op jit(solution)/shard_map/pallas_call | solution.py:359
  1.8 4.9 %shard_map.201 = (f32[256,256]{1,0:T(8,128)S(1)}, f32[4,256,256]{2,1,0:T(8,128)S(1)}, f32[4,256,256]{2,1,0:T(8,128)S(1)}, f32[256,256]{1,0:T(8,128)S(1)}) custom-call(f32[16,256,256]{2,1,0:T(8,128)} %refs_1_.11), custom_call_target="tpu_custom_call" | custom-call | tf_op jit(solution)/shard_map/pallas_call | solution.py:359
  6.8 4.1 %collective-permute-start.2 = (f32[256,256]{1,0:T(8,128)S(1)}, f32[256,256]{1,0:T(8,128)S(1)}, u32[]{:S(2)}, u32[]{:S(2)}) collective-permute-start(f32[256,256]{1,0:T(8,128)S(1)} %get-tuple-element.50.refs_1_), channel_id=1, source_target_pairs={{0,4},{2,6},{4,0},{6,2},{1,5},{3,7},{5,1},{7,3},{8,12},{10,14},{12... | collective-permute-start | bytes 786440 | tf_op jit(solution)/shard_map/ppermute | solution.py:375
  10.9 0.7 collective-permute-start.1
  11.6 1.3 %collective-permute-start = (f32[256,256]{1,0:T(8,128)S(1)}, f32[256,256]{1,0:T(8,128)S(1)}, u32[]{:S(2)}, u32[]{:S(2)}) collective-permute-start(f32[256,256]{1,0:T(8,128)S(1)} %get-tuple-element.50.refs_1_), channel_id=1, source_target_pairs={{0,2},{2,4},{4,6},{6,0},{1,3},{3,5},{5,7},{7,1},{8,10},{10,12},{12... | collective-permute-start | bytes 786440 | tf_op jit(solution)/shard_map/ppermute | solution.py:375
  12.9 0.1 pad_add_fusion.refs_0_
  13.0 1.3 %collective-permute-start.4 = (f32[8,256]{1,0:T(8,128)S(1)}, f32[8,256]{1,0:T(8,128)S(1)}, u32[]{:S(2)}, u32[]{:S(2)}) collective-permute-start(f32[8,256]{1,0:T(8,128)S(1)} %slice.3), channel_id=1, source_target_pairs={{2,0},{4,2},{6,4},{8,6},{10,8},{12,10},{14,12},{16,14},{18,16},{20... | collective-permute-start | bytes 24584 | tf_op jit(solution)/shard_map/ppermute | solution.py:382
  14.3 4.5 %collective-permute-start.3 = (f32[8,256]{1,0:T(8,128)S(1)}, f32[8,256]{1,0:T(8,128)S(1)}, u32[]{:S(2)}, u32[]{:S(2)}) collective-permute-start(f32[8,256]{1,0:T(8,128)S(1)} %shard_map.200), channel_id=1, source_target_pairs={{0,2},{2,4},{4,6},{6,8},{8,10},{10,12},{12,14},{14,16},{16,18},{18... | collective-permute-start | bytes 24584 | tf_op jit(solution)/shard_map/ppermute | solution.py:382
  18.8 4.9 %collective-permute-done.4.refs_18_ = f32[8,256]{1,0:T(8,128)S(1)} collective-permute-done((f32[8,256]{1,0:T(8,128)S(1)}, f32[8,256]{1,0:T(8,128)S(1)}, u32[]{:S(2)}, u32[]{:S(2)}) %collective-permute-start.4) | collective-permute-done | bytes 8224 | tf_op jit(solution)/shard_map/ppermute | solution.py:382
  23.7 0.0 collective-permute-done.3.refs_17_
  23.7 8.3 %shard_map.202 = (f32[16,256]{1,0:T(8,128)S(1)}, f32[16,64]{1,0:T(8,128)S(1)}, f32[16,256]{1,0:T(8,128)S(1)}, f32[16,256]{1,0:T(8,128)S(1)}, f32[8,256]{1,0:T(8,128)S(1)}, /*index=5*/f32[8,128]{1,0:T(8,128)S(1)}) custom-call(f32[16,256,256]{2,1,0:T(8,128)} %refs_0_.5, f32[16,64,256]{2,1,0:T(8,128)} %refs_1_.10, f32[16,256,256]{2,1,0:T(8,128)} %refs_2_.11, ...), custom_call_target="tpu_custom_call" | custom-call | tf_op jit(solution)/shard_map/pallas_call | solution.py:359
  32.0 2.5 %collective-permute-start.7 = (f32[8,256]{1,0:T(8,128)S(1)}, f32[8,256]{1,0:T(8,128)S(1)}, u32[]{:S(2)}, u32[]{:S(2)}) collective-permute-start(f32[8,256]{1,0:T(8,128)S(1)} %get-tuple-element.54.refs_5_), channel_id=1, source_target_pairs={{0,4},{2,6},{4,0},{6,2},{1,5},{3,7},{5,1},{7,3},{8,12},{10,14},{12... | collective-permute-start | bytes 24584 | tf_op jit(solution)/shard_map/ppermute | solution.py:375
  34.6 1.2 %collective-permute-start.6 = (f32[8,256]{1,0:T(8,128)S(1)}, f32[8,256]{1,0:T(8,128)S(1)}, u32[]{:S(2)}, u32[]{:S(2)}) collective-permute-start(f32[8,256]{1,0:T(8,128)S(1)} %get-tuple-element.54.refs_5_), channel_id=1, source_target_pairs={{0,6},{2,0},{4,2},{6,4},{1,7},{3,1},{5,3},{7,5},{8,14},{10,8},{12,... | collective-permute-start | bytes 24584 | tf_op jit(solution)/shard_map/ppermute | solution.py:375
  35.8 1.5 %collective-permute-done.7.refs_8_ = f32[8,256]{1,0:T(8,128)S(1)} collective-permute-done((f32[8,256]{1,0:T(8,128)S(1)}, f32[8,256]{1,0:T(8,128)S(1)}, u32[]{:S(2)}, u32[]{:S(2)}) %collective-permute-start.7) | collective-permute-done | bytes 8224 | tf_op jit(solution)/shard_map/ppermute | solution.py:375
  37.3 1.0 collective-permute-start.5
  38.3 0.0 collective-permute-done.6.refs_7_
  38.3 3.9 %collective-permute-done.5.refs_6_ = f32[8,256]{1,0:T(8,128)S(1)} collective-permute-done((f32[8,256]{1,0:T(8,128)S(1)}, f32[8,256]{1,0:T(8,128)S(1)}, u32[]{:S(2)}, u32[]{:S(2)}) %collective-permute-start.5) | collective-permute-done | bytes 8224 | tf_op jit(solution)/shard_map/ppermute | solution.py:375
  42.1 0.0 collective-permute-done.2.refs_4_
  42.2 0.7 copy-done.11
  42.9 0.0 collective-permute-done.1.refs_3_
  42.9 0.7 copy-done.13
  43.6 0.7 copy-done.15
  44.3 0.9 copy-done.10
  45.3 0.9 copy-done.12
  46.2 0.9 copy-done.14
  47.2 0.9 copy-done.16
  48.1 1.5 %shard_map.203 = (f32[4,256,256]{2,1,0:T(8,128)S(1)}, f32[4,8,256]{2,1,0:T(8,128)S(1)}, f32[264,256]{1,0:T(8,128)S(1)}) custom-call(s32[3]{0:T(128)S(1)} %pad_add_fusion.refs_0_, f32[256,256]{1,0:T(8,128)S(1)} %copy-done.10, f32[256,256]{1,0:T(8,128)S(1)} %copy-done.16, f32[256,256]{1,0:T(8,128)S(1)} %copy-done.14, f32[256,256]{1,0:T(8,128)S(1)} %copy-done.12, ...), custom_call_target="tpu_custom_call" | custom-call | tf_op jit(solution)/shard_map/pallas_call | solution.py:359
  49.7 3.8 %collective-permute-start.10 = (f32[264,256]{1,0:T(8,128)S(1)}, f32[264,256]{1,0:T(8,128)S(1)}, u32[]{:S(2)}, u32[]{:S(2)}) collective-permute-start(f32[264,256]{1,0:T(8,128)S(1)} %get-tuple-element.56.refs_1_), channel_id=1, source_target_pairs={{0,16},{8,24},{16,0},{24,8},{1,17},{9,25},{17,1},{25,9},{2,18},{10... | collective-permute-start | bytes 811016 | tf_op jit(solution)/shard_map/ppermute | solution.py:375
  53.5 1.1 %collective-permute-start.9 = (f32[264,256]{1,0:T(8,128)S(1)}, f32[264,256]{1,0:T(8,128)S(1)}, u32[]{:S(2)}, u32[]{:S(2)}) collective-permute-start(f32[264,256]{1,0:T(8,128)S(1)} %get-tuple-element.56.refs_1_), channel_id=1, source_target_pairs={{0,24},{8,0},{16,8},{24,16},{1,25},{9,1},{17,9},{25,17},{2,26},{10... | collective-permute-start | bytes 811016 | tf_op jit(solution)/shard_map/ppermute | solution.py:375
  54.6 0.9 collective-permute-start.8
  55.5 6.8 %shard_map.204 = (f32[256,256]{1,0:T(8,128)S(1)}, f32[256,256]{1,0:T(8,128)S(1)}) custom-call(f32[16,256,256]{2,1,0:T(8,128)} %refs_1_.11, f32[16,64,256]{2,1,0:T(8,128)} %refs_1_.10, f32[16,64,64]{2,1,0:T(8,128)} %refs_2_.10, f32[4,256,256]{2,1,0:T(8,128)S(1)} %get-tuple-element.58.refs_3_, ...), custom_call_target="tpu_custom_call" | custom-call | tf_op jit(solution)/shard_map/pallas_call | solution.py:359
  62.3 0.2 collective-permute-done.9.refs_3_
  62.5 0.2 collective-permute-done.8.refs_2_
  62.8 1.6 %shard_map.205 = (f32[4,256,256]{2,1,0:T(8,128)S(1)}, f32[4,8,256]{2,1,0:T(8,128)S(1)}, f32[264,256]{1,0:T(8,128)S(1)}) custom-call(s32[3]{0:T(128)S(1)} %pad_add_fusion.refs_0_, f32[264,256]{1,0:T(8,128)S(1)} %get-tuple-element.56.refs_1_, f32[264,256]{1,0:T(8,128)S(1)} %collective-permute-done.8.refs_2_, f32[264,256]{1,0:T(8,128)S(1)} %collective-permute-done.9.refs_3_, ...), custom_call_target="tpu_custom_call" | custom-call | tf_op jit(solution)/shard_map/pallas_call | solution.py:359
  64.3 6.1 %collective-permute-start.13 = (f32[264,256]{1,0:T(8,128)S(1)}, f32[264,256]{1,0:T(8,128)S(1)}, u32[]{:S(2)}, u32[]{:S(2)}) collective-permute-start(f32[264,256]{1,0:T(8,128)S(1)} %get-tuple-element.65.refs_1_.refs_8_), channel_id=1, source_target_pairs={{0,64},{32,96},{64,0},{96,32},{1,65},{33,97},{65,1},{97,33},{2,66}... | collective-permute-start | bytes 811016 | tf_op jit(solution)/shard_map/ppermute | solution.py:375
  70.5 1.1 collective-permute-start.12
  71.5 1.0 collective-permute-start.11
  72.5 7.8 %shard_map.206 = (f32[16,256]{1,0:T(8,128)}, f32[16,64]{1,0:T(8,128)}, f32[16,64]{1,0:T(8,128)}, f32[16,256]{1,0:T(8,128)}, f32[8,256]{1,0:T(8,128)}, /*index=5*/f32[8,256]{1,0:T(8,128)S(1)}) custom-call(f32[16,256,256]{2,1,0:T(8,128)} %refs_1_.11, f32[16,64,256]{2,1,0:T(8,128)} %refs_1_.10, f32[16,64,64]{2,1,0:T(8,128)} %refs_2_.10, ...), custom_call_target="tpu_custom_call" | custom-call | tf_op jit(solution)/shard_map/pallas_call | solution.py:359
  80.3 0.6 copy-done.17
  80.9 0.6 copy-done.18
  81.5 0.6 copy-done.19
  82.1 0.6 copy-done.20
  82.8 4.2 %shard_map.207 = (f32[8,256]{1,0:T(8,128)}, f32[64,1,384]{2,1,0:T(1,128)}) custom-call(s32[3]{0:T(128)S(1)} %pad_add_fusion.refs_0_, f32[264,256]{1,0:T(8,128)S(1)} %get-tuple-element.65.refs_1_.refs_8_, f32[264,256]{1,0:T(8,128)S(1)} %collective-permute-done.11.refs_2_.refs_9_, f32[264,256]{1,0:T(8,128)S(1)} %collective-permute-done.12.refs_3_.refs_10_, ...), custom_call_target="tpu_custom_call" | custom-call | tf_op jit(solution)/shard_map/pallas_call | solution.py:359
  87.0 5.6 %all-to-all-start = ((f32[64,1,384]{2,1,0:T(1,128)}), f32[64,1,384]{2,1,0:T(1,128)S(1)}, u32[]{:S(2)}, u32[]{:S(2)}) async-start(f32[64,1,384]{2,1,0:T(1,128)} %get-tuple-element.85), calls=%async_computation | async-start | bytes 196608 | tf_op jit(solution)/shard_map/all_to_all | solution.py:468
  92.7 8.4 %shard_map.208 = (f32[16,256]{1,0:T(8,128)}, f32[16,64]{1,0:T(8,128)}, f32[16,64]{1,0:T(8,128)}, f32[16,256]{1,0:T(8,128)}, f32[8,256]{1,0:T(8,128)}, /*index=5*/f32[8,256]{1,0:T(8,128)}) custom-call(f32[16,256,256]{2,1,0:T(8,128)} %refs_1_.11, f32[16,64,256]{2,1,0:T(8,128)} %refs_1_.10, f32[16,64,64]{2,1,0:T(8,128)} %refs_2_.10, f32[4,256,256]{2,1,0:T(8,128)} %copy-done, ...), custom_call_target="tpu_custom_call" | custom-call | tf_op jit(solution)/shard_map/pallas_call | solution.py:359
  101.0 1.1 %all-to-all-done.refs_23_ = f32[64,1,384]{2,1,0:T(1,128)S(1)} async-done(((f32[64,1,384]{2,1,0:T(1,128)}), f32[64,1,384]{2,1,0:T(1,128)S(1)}, u32[]{:S(2)}, u32[]{:S(2)}) %all-to-all-start) | async-done | bytes 98336 | tf_op jit(solution)/shard_map/all_to_all | solution.py:468
  102.2 8.4 %shard_map.209 = (f32[16,256]{1,0:T(8,128)}, f32[16,64]{1,0:T(8,128)}, f32[16,256]{1,0:T(8,128)}, f32[16,64]{1,0:T(8,128)}, f32[1,3]{1,0:T(1,128)}) custom-call(s32[3]{0:T(128)S(1)} %pad_add_fusion.refs_0_, f32[16,256,256]{2,1,0:T(8,128)} %refs_1_.11, f32[16,256,256]{2,1,0:T(8,128)} %refs_2_.11, f32[16,64,256]{2,1,0:T(8,128)} %refs_3_.5, s32[16,64]{1,0:T(8,128)} %refs_4_.3, ...), custom_call_target="tpu_custom_call" | custom-call | tf_op jit(solution)/shard_map/pallas_call | solution.py:359
  (38 shorter events, 0.1 us)
Async XLA Ops:
  0.6 12.3 %copy-start.21 = (f32[16,256]{1,0:T(8,128)S(1)}, f32[16,256]{1,0:T(8,128)}, u32[]{:S(2)}) copy-start(f32[16,256]{1,0:T(8,128)} %refs_7_.2) | copy-start | bytes 49156
  6.8 25.3 %copy-start.9 = (f32[256,256]{1,0:T(8,128)}, f32[256,256]{1,0:T(8,128)S(1)}, u32[]{:S(2)}) copy-start(f32[256,256]{1,0:T(8,128)S(1)} %get-tuple-element.50.refs_1_) | copy-start | bytes 786436
  6.8 48.7 %copy-start.3 = (f32[256,256]{1,0:T(8,128)}, f32[256,256]{1,0:T(8,128)S(1)}, u32[]{:S(2)}) copy-start(f32[256,256]{1,0:T(8,128)S(1)} %get-tuple-element.52.refs_16_.refs_5_.refs_15_) | copy-start | bytes 786436
  6.8 65.7 %copy-start = (f32[4,256,256]{2,1,0:T(8,128)}, f32[4,256,256]{2,1,0:T(8,128)S(1)}, u32[]{:S(2)}) copy-start(f32[4,256,256]{2,1,0:T(8,128)S(1)} %get-tuple-element.51.refs_15_.refs_4_.refs_3_.refs_14_) | copy-start | bytes 3145732
  6.8 35.4 %collective-permute-start.2 = (f32[256,256]{1,0:T(8,128)S(1)}, f32[256,256]{1,0:T(8,128)S(1)}, u32[]{:S(2)}, u32[]{:S(2)}) collective-permute-start(f32[256,256]{1,0:T(8,128)S(1)} %get-tuple-element.50.refs_1_), channel_id=1, source_target_pairs={{0,4},{2,6},{4,0},{6,2},{1,5},{3,7},{5,1},{7,3},{8,12},{10,14},{12... | collective-permute-start | bytes 786440 | tf_op jit(solution)/shard_map/ppermute | solution.py:375
  10.9 32.0 %collective-permute-start.1 = (f32[256,256]{1,0:T(8,128)S(1)}, f32[256,256]{1,0:T(8,128)S(1)}, u32[]{:S(2)}, u32[]{:S(2)}) collective-permute-start(f32[256,256]{1,0:T(8,128)S(1)} %get-tuple-element.50.refs_1_), channel_id=1, source_target_pairs={{0,6},{2,0},{4,2},{6,4},{1,7},{3,1},{5,3},{7,5},{8,14},{10,8},{12,... | collective-permute-start | bytes 786440 | tf_op jit(solution)/shard_map/ppermute | solution.py:375
  11.6 32.0 %collective-permute-start = (f32[256,256]{1,0:T(8,128)S(1)}, f32[256,256]{1,0:T(8,128)S(1)}, u32[]{:S(2)}, u32[]{:S(2)}) collective-permute-start(f32[256,256]{1,0:T(8,128)S(1)} %get-tuple-element.50.refs_1_), channel_id=1, source_target_pairs={{0,2},{2,4},{4,6},{6,0},{1,3},{3,5},{5,7},{7,1},{8,10},{10,12},{12... | collective-permute-start | bytes 786440 | tf_op jit(solution)/shard_map/ppermute | solution.py:375
  13.0 10.8 %collective-permute-start.4 = (f32[8,256]{1,0:T(8,128)S(1)}, f32[8,256]{1,0:T(8,128)S(1)}, u32[]{:S(2)}, u32[]{:S(2)}) collective-permute-start(f32[8,256]{1,0:T(8,128)S(1)} %slice.3), channel_id=1, source_target_pairs={{2,0},{4,2},{6,4},{8,6},{10,8},{12,10},{14,12},{16,14},{18,16},{20... | collective-permute-start | bytes 24584 | tf_op jit(solution)/shard_map/ppermute | solution.py:382
  14.3 9.5 %collective-permute-start.3 = (f32[8,256]{1,0:T(8,128)S(1)}, f32[8,256]{1,0:T(8,128)S(1)}, u32[]{:S(2)}, u32[]{:S(2)}) collective-permute-start(f32[8,256]{1,0:T(8,128)S(1)} %shard_map.200), channel_id=1, source_target_pairs={{0,2},{2,4},{4,6},{6,8},{8,10},{10,12},{12,14},{14,16},{16,18},{18... | collective-permute-start | bytes 24584 | tf_op jit(solution)/shard_map/ppermute | solution.py:382
  32.0 5.2 %collective-permute-start.7 = (f32[8,256]{1,0:T(8,128)S(1)}, f32[8,256]{1,0:T(8,128)S(1)}, u32[]{:S(2)}, u32[]{:S(2)}) collective-permute-start(f32[8,256]{1,0:T(8,128)S(1)} %get-tuple-element.54.refs_5_), channel_id=1, source_target_pairs={{0,4},{2,6},{4,0},{6,2},{1,5},{3,7},{5,1},{7,3},{8,12},{10,14},{12... | collective-permute-start | bytes 24584 | tf_op jit(solution)/shard_map/ppermute | solution.py:375
  34.6 3.7 %collective-permute-start.6 = (f32[8,256]{1,0:T(8,128)S(1)}, f32[8,256]{1,0:T(8,128)S(1)}, u32[]{:S(2)}, u32[]{:S(2)}) collective-permute-start(f32[8,256]{1,0:T(8,128)S(1)} %get-tuple-element.54.refs_5_), channel_id=1, source_target_pairs={{0,6},{2,0},{4,2},{6,4},{1,7},{3,1},{5,3},{7,5},{8,14},{10,8},{12,... | collective-permute-start | bytes 24584 | tf_op jit(solution)/shard_map/ppermute | solution.py:375
  37.3 4.9 %collective-permute-start.5 = (f32[8,256]{1,0:T(8,128)S(1)}, f32[8,256]{1,0:T(8,128)S(1)}, u32[]{:S(2)}, u32[]{:S(2)}) collective-permute-start(f32[8,256]{1,0:T(8,128)S(1)} %get-tuple-element.54.refs_5_), channel_id=1, source_target_pairs={{0,2},{2,4},{4,6},{6,0},{1,3},{3,5},{5,7},{7,1},{8,10},{10,12},{12... | collective-permute-start | bytes 24584 | tf_op jit(solution)/shard_map/ppermute | solution.py:375
  42.2 0.7 copy-start.11
  42.9 0.7 copy-start.13
  43.6 0.7 copy-start.15
  44.3 0.9 copy-start.10
  45.3 0.9 copy-start.12
  46.2 0.9 copy-start.14
  47.2 0.9 copy-start.16
  49.6 33.1 %copy-start.1 = (f32[4,256,256]{2,1,0:T(8,128)}, f32[4,256,256]{2,1,0:T(8,128)S(1)}, u32[]{:S(2)}) copy-start(f32[4,256,256]{2,1,0:T(8,128)S(1)} %get-tuple-element.67.refs_7_.refs_13_) | copy-start | bytes 3145732
  49.7 12.7 %collective-permute-start.10 = (f32[264,256]{1,0:T(8,128)S(1)}, f32[264,256]{1,0:T(8,128)S(1)}, u32[]{:S(2)}, u32[]{:S(2)}) collective-permute-start(f32[264,256]{1,0:T(8,128)S(1)} %get-tuple-element.56.refs_1_), channel_id=1, source_target_pairs={{0,16},{8,24},{16,0},{24,8},{1,17},{9,25},{17,1},{25,9},{2,18},{10... | collective-permute-start | bytes 811016 | tf_op jit(solution)/shard_map/ppermute | solution.py:375
  53.5 9.1 %collective-permute-start.9 = (f32[264,256]{1,0:T(8,128)S(1)}, f32[264,256]{1,0:T(8,128)S(1)}, u32[]{:S(2)}, u32[]{:S(2)}) collective-permute-start(f32[264,256]{1,0:T(8,128)S(1)} %get-tuple-element.56.refs_1_), channel_id=1, source_target_pairs={{0,24},{8,0},{16,8},{24,16},{1,25},{9,1},{17,9},{25,17},{2,26},{10... | collective-permute-start | bytes 811016 | tf_op jit(solution)/shard_map/ppermute | solution.py:375
  54.6 8.2 %collective-permute-start.8 = (f32[264,256]{1,0:T(8,128)S(1)}, f32[264,256]{1,0:T(8,128)S(1)}, u32[]{:S(2)}, u32[]{:S(2)}) collective-permute-start(f32[264,256]{1,0:T(8,128)S(1)} %get-tuple-element.56.refs_1_), channel_id=1, source_target_pairs={{0,8},{8,16},{16,24},{24,0},{1,9},{9,17},{17,25},{25,1},{2,10},{10... | collective-permute-start | bytes 811016 | tf_op jit(solution)/shard_map/ppermute | solution.py:375
  62.3 24.7 %copy-start.8 = (f32[256,256]{1,0:T(8,128)}, f32[256,256]{1,0:T(8,128)S(1)}, u32[]{:S(2)}) copy-start(f32[256,256]{1,0:T(8,128)S(1)} %get-tuple-element.68.refs_16_) | copy-start | bytes 786436
  64.3 22.6 %copy-start.2 = (f32[4,256,256]{2,1,0:T(8,128)}, f32[4,256,256]{2,1,0:T(8,128)S(1)}, u32[]{:S(2)}) copy-start(f32[4,256,256]{2,1,0:T(8,128)S(1)} %get-tuple-element.66.refs_5_.refs_12_) | copy-start | bytes 3145732
  64.3 22.6 %copy-start.4 = (f32[264,256]{1,0:T(8,128)}, f32[264,256]{1,0:T(8,128)S(1)}, u32[]{:S(2)}) copy-start(f32[264,256]{1,0:T(8,128)S(1)} %get-tuple-element.65.refs_1_.refs_8_) | copy-start | bytes 811012
  64.3 18.4 %collective-permute-start.13 = (f32[264,256]{1,0:T(8,128)S(1)}, f32[264,256]{1,0:T(8,128)S(1)}, u32[]{:S(2)}, u32[]{:S(2)}) collective-permute-start(f32[264,256]{1,0:T(8,128)S(1)} %get-tuple-element.65.refs_1_.refs_8_), channel_id=1, source_target_pairs={{0,64},{32,96},{64,0},{96,32},{1,65},{33,97},{65,1},{97,33},{2,66}... | collective-permute-start | bytes 811016 | tf_op jit(solution)/shard_map/ppermute | solution.py:375
  70.5 12.2 %collective-permute-start.12 = (f32[264,256]{1,0:T(8,128)S(1)}, f32[264,256]{1,0:T(8,128)S(1)}, u32[]{:S(2)}, u32[]{:S(2)}) collective-permute-start(f32[264,256]{1,0:T(8,128)S(1)} %get-tuple-element.65.refs_1_.refs_8_), channel_id=1, source_target_pairs={{0,96},{32,0},{64,32},{96,64},{1,97},{33,1},{65,33},{97,65},{2,98}... | collective-permute-start | bytes 811016 | tf_op jit(solution)/shard_map/ppermute | solution.py:375
  71.5 11.2 %collective-permute-start.11 = (f32[264,256]{1,0:T(8,128)S(1)}, f32[264,256]{1,0:T(8,128)S(1)}, u32[]{:S(2)}, u32[]{:S(2)}) collective-permute-start(f32[264,256]{1,0:T(8,128)S(1)} %get-tuple-element.65.refs_1_.refs_8_), channel_id=1, source_target_pairs={{0,32},{32,64},{64,96},{96,0},{1,33},{33,65},{65,97},{97,1},{2,34}... | collective-permute-start | bytes 811016 | tf_op jit(solution)/shard_map/ppermute | solution.py:375
  80.3 0.6 copy-start.17
  80.9 0.6 copy-start.18
  81.5 0.6 copy-start.19
  82.1 0.6 copy-start.20
  82.7 4.3 %copy-start.5 = (f32[264,256]{1,0:T(8,128)}, f32[264,256]{1,0:T(8,128)S(1)}, u32[]{:S(2)}) copy-start(f32[264,256]{1,0:T(8,128)S(1)} %collective-permute-done.13.refs_4_.refs_11_) | copy-start | bytes 811012
  82.7 4.3 %copy-start.6 = (f32[264,256]{1,0:T(8,128)}, f32[264,256]{1,0:T(8,128)S(1)}, u32[]{:S(2)}) copy-start(f32[264,256]{1,0:T(8,128)S(1)} %collective-permute-done.12.refs_3_.refs_10_) | copy-start | bytes 811012
  82.7 4.3 %copy-start.7 = (f32[264,256]{1,0:T(8,128)}, f32[264,256]{1,0:T(8,128)S(1)}, u32[]{:S(2)}) copy-start(f32[264,256]{1,0:T(8,128)S(1)} %collective-permute-done.11.refs_2_.refs_9_) | copy-start | bytes 811012
  87.0 15.2 %all-to-all-start = ((f32[64,1,384]{2,1,0:T(1,128)}), f32[64,1,384]{2,1,0:T(1,128)S(1)}, u32[]{:S(2)}, u32[]{:S(2)}) async-start(f32[64,1,384]{2,1,0:T(1,128)} %get-tuple-element.85), calls=%async_computation | async-start | bytes 196608 | tf_op jit(solution)/shard_map/all_to_all | solution.py:468

commit v2 on v1

v2 whole, which is shorter than its diff:
```python
import functools

import jax
import jax.numpy as jnp
from jax import lax
from jax.experimental import pallas as pl
from jax.experimental.pallas import tpu as pltpu
from jax.sharding import Mesh
from jax.sharding import PartitionSpec as P

TM = ("tm_0", "tm_1", "tm_2")
BATCH_TM = ("batch", "tm_0", "tm_1", "tm_2")
F32 = jnp.float32
BF16 = jnp.bfloat16
floor_share = 0.001
VMEM = pltpu.VMEM
SMEM = pltpu.SMEM


def halves(x):
    high = x.astype(BF16)
    low = (x - high.astype(F32)).astype(BF16)
    return high, low


def dot(a, b, ca, cb):
    return lax.dot_general(a, b, (((ca,), (cb,)), ((), ())), preferred_element_type=F32)


def mat_mul(a, b, ca=1, cb=0):
    ah, al = halves(a)
    bh, bl = halves(b)
    return dot(ah, bh, ca, cb) + (dot(ah, bl, ca, cb) + dot(al, bh, ca, cb))


def row_halves(v):
    high = v.astype(BF16).astype(F32)
    row = lax.broadcasted_iota(jnp.int32, (8, v.shape[1]), 0)
    both = jnp.where(row == 0, high, jnp.where(row == 1, v - high, 0.0))
    return both.astype(BF16)


def vec_mat(v, m, cb=0):
    lhs = row_halves(v)
    mh, ml = halves(m)
    r = dot(lhs, mh, 1, cb) + dot(lhs, ml, 1, cb)
    return jnp.sum(r, axis=0, keepdims=True)


def last_prediction_body(ready, f_ref, m_ref, x_ref, u_ref, out_ref):
    ready(0)
    v = vec_mat(x_ref[7:8, :], f_ref[0], 1) + vec_mat(u_ref[7:8, :], m_ref[0])
    out_ref[...] = jnp.broadcast_to(v, (8, 256))


def block_product_body(*refs, sections, rows):
    n = len(sections)
    far = refs[: n + rows]
    p_ref, pair_ref, quad_ref, half_ref = refs[n + rows: n + rows + 4]
    kept = refs[n + rows + 4: 2 * (n + rows) + 4]
    low_ref, sems = refs[2 * (n + rows) + 4:]
    a_ref = kept[0]
    loops = [
        pltpu.make_async_copy(far[0].at[pl.ds(4 * j, 4)], a_ref.at[pl.ds(4 * j, 4)], sems.at[j]) for j in range(4)
    ]
    rest = [pltpu.make_async_copy(f, k, sems.at[4 + i]) for i, (f, k) in enumerate(zip(far[1:], kept[1:]))]
    for move in loops + rest:
        move.start()
    for j in range(5):
        if j < 4:
            loops[j].wait()
            low_ref[j] = mat_mul(a_ref[4 * j + 1], a_ref[4 * j])
            pair_ref[j] = mat_mul(a_ref[4 * j + 3], a_ref[4 * j + 2])
        if j == 3:
            half_ref[...] = mat_mul(quad_ref[1], quad_ref[0])
        if j > 0:
            quad_ref[j - 1] = mat_mul(pair_ref[j - 1], low_ref[j - 1])
    p_ref[...] = mat_mul(mat_mul(quad_ref[3], quad_ref[2]), half_ref[...])
    for move in rest:
        move.wait()


def total(x):
    return jnp.sum(jnp.sum(x, axis=0, keepdims=True), axis=1, keepdims=True)


def sources_body(
    ready, f_ref, m_ref, v_ref, k_ref, a_ref,
    x_ref, u_ref, mult_ref, bm_ref, ub_ref, off_ref, sw_ref, sl_ref, il_ref, iw_ref,
    quad_ref, half_ref, p_ref, before_ref, next_ref,
    defect_ref, gi_ref, src_ref, b_ref, out_ref, stat_ref,
    gs_ref,
):
    gi_ref[...] = mat_mul(u_ref[...], iw_ref[...], 1, 1) + il_ref[...] + bm_ref[...]
    gs_ref[...] = sw_ref[...] * x_ref[...] + sl_ref[...] + mult_ref[...]
    src_ref[...] = x_ref[...] - off_ref[...]
    prev = before_ref[0:1, :]
    for i in range(4):
        for j in range(4):
            k = i * 4 + j
            follow = next_ref[0:1, :] if k == 15 else mult_ref[k + 1:k + 2, :]
            gs = gs_ref[k:k + 1, :] - vec_mat(follow, f_ref[k])
            gs_ref[k:k + 1, :] = gs
            gi = gi_ref[k:k + 1, :] - vec_mat(follow, m_ref[k], 1)
            gi_ref[k:k + 1, :] = gi
            d = src_ref[k:k + 1, :] - prev
            defect_ref[k:k + 1, :] = d
            src_ref[k:k + 1, :] = vec_mat(d, v_ref[k]) + gs + vec_mat(gi, k_ref[k])
            if k < 15:
                prev = vec_mat(x_ref[k:k + 1, :], f_ref[k], 1) + vec_mat(u_ref[k:k + 1, :], m_ref[k])
    b = [src_ref[4 * j + 3:4 * j + 4, :] for j in range(4)]
    for j in range(4):
        b_ref[4 * j + 3:4 * j + 4, :] = b[j]
    for m in (2, 1, 0):
        for j in range(4):
            k = 4 * j + m
            b[j] = vec_mat(b[j], a_ref[k]) + src_ref[k:k + 1, :]
            b_ref[k:k + 1, :] = b[j]
    upper = b[2] + vec_mat(b[3], quad_ref[2])
    c = b[0] + vec_mat(b[1], quad_ref[0]) + vec_mat(upper, half_ref[...])
    out_ref[0:256, :] = p_ref[...]
    out_ref[256:264, :] = jnp.broadcast_to(c, (8, 256))

    gap = bm_ref[...] * (ub_ref[...] - u_ref[...])
    d, gs, gi = defect_ref[...], gs_ref[...], gi_ref[...]
    off, sl, il, bm = off_ref[...], sl_ref[...], il_ref[...], bm_ref[...]
    found = (
        total(d * d),
        total(gs * gs) + total(gi * gi),
        total(gap * gap),
        total(off * off),
        total(sl * sl) + total(il * il),
        total(bm * bm),
    )
    lane = lax.broadcasted_iota(jnp.int32, (8, 128), 1)
    out = jnp.zeros((8, 128), F32)
    for n, s in enumerate(found):
        out = jnp.where(lane == n, s, out)
    stat_ref[...] = out


def weight_body(ready, a_ref, m_ref, g_ref, pair_ref, quad_ref, half_ref, w_ref, third_ref, b_ref, gb_ref):
    third_ref[...] = mat_mul(quad_ref[2], half_ref[...])
    for j in range(4):
        k = 4 * j
        r = 256 * j
        b_ref[r:r + 64, :] = mat_mul(m_ref[k], a_ref[k + 1], 1, 1)
        b_ref[r + 64:r + 128, :] = m_ref[k + 1]
        b_ref[r + 128:r + 192, :] = mat_mul(m_ref[k + 2], a_ref[k + 3], 1, 1)
        b_ref[r + 192:r + 256, :] = m_ref[k + 3]
        b_ref[r:r + 128, :] = mat_mul(b_ref[r:r + 128, :], pair_ref[j], 1, 1)
    for j in (1, 2, 3):
        b_ref[0:256 * j, :] = mat_mul(b_ref[0:256 * j, :], quad_ref[j], 1, 1)
    for k in range(16):
        gb_ref[64 * k:64 * k + 64, :] = mat_mul(g_ref[k], b_ref[64 * k:64 * k + 64, :])
    w_ref[...] = mat_mul(b_ref[...], gb_ref[...], 0, 0)


def backward_part(a_ref, m_ref, g_ref, quad_ref, b_ref, src_ref, gi_ref, lam, before_ref, gain_ref, base_ref, push_ref, after_ref, loaded=lambda: None):
    lams = [None, None, None, lam]
    for j in (2, 1, 0):
        known = b_ref[4 * j + 4:4 * j + 5, :]
        lams[j] = known if lams[j + 1] is None else vec_mat(lams[j + 1], quad_ref[j + 1]) + known
    before_ref[0:1, :] = vec_mat(lams[0], quad_ref[0]) + b_ref[0:1, :]
    for j in range(3):
        before_ref[4 * j + 4:4 * j + 5, :] = lams[j]
    loaded()
    for m in (3, 2, 1, 0):
        for j in range(4):
            k = 4 * j + m
            now = lams[j]
            after_ref[k:k + 1, :] = jnp.zeros((1, 256), F32) if now is None else now
            if m > 0:
                lams[j] = src_ref[k:k + 1, :] if now is None else vec_mat(now, a_ref[k]) + src_ref[k:k + 1, :]
                before_ref[k:k + 1, :] = lams[j]
    for k in range(16):
        base = gi_ref[k:k + 1, :] + vec_mat(after_ref[k:k + 1, :], m_ref[k], 1)
        base_ref[k:k + 1, :] = base
        gain = -vec_mat(base, g_ref[k])
        gain_ref[k:k + 1, :] = gain
        push_ref[k:k + 1, :] = vec_mat(gain, m_ref[k])


def local_ends(a_ref, push_ref, defect_ref):
    ends = [None] * 4
    for m in range(4):
        for j in range(4):
            k = 4 * j + m
            step = -defect_ref[k:k + 1, :] if m == 0 else ends[j] - defect_ref[k:k + 1, :]
            ends[j] = vec_mat(step, a_ref[k], 1) + push_ref[k:k + 1, :]
    return ends


def local_body(
    ready, a_ref, m_ref, g_ref, quad_ref, b_ref, src_ref, gi_ref, defect_ref,
    end_ref, before_ref, gain_ref, base_ref, push_ref, after_ref,
):
    backward_part(
        a_ref, m_ref, g_ref, quad_ref, b_ref, src_ref, gi_ref, None,
        before_ref, gain_ref, base_ref, push_ref, after_ref,
    )
    ends = local_ends(a_ref, push_ref, defect_ref)
    e = ends[0]
    for j in (1, 2, 3):
        e = vec_mat(e, quad_ref[j], 1) + ends[j]
    end_ref[...] = jnp.broadcast_to(e, (8, 256))


def order(ref, place, own, minus, plus, across):
    ref[place] = own
    ref[lax.rem(place + 1, 4)] = plus
    ref[lax.rem(place + 2, 4)] = across
    ref[lax.rem(place + 3, 4)] = minus


def join_body(ready, idx_ref, *refs, axis):
    place = idx_ref[axis]
    maps_ref, vectors_ref, out_ref = refs[-3:]
    parts = refs[:4]
    order(maps_ref, place, *[r[0:256, :] for r in parts])
    order(vectors_ref, place, *[r[256:264, :] for r in parts])
    high = mat_mul(maps_ref[3], maps_ref[2])
    low = mat_mul(maps_ref[1], maps_ref[0])
    v = vectors_ref[3, 0:1, :]
    for j in (2, 1, 0):
        v = vec_mat(v, maps_ref[j]) + vectors_ref[j, 0:1, :]
    out_ref[0:256, :] = mat_mul(high, low)
    out_ref[256:264, :] = jnp.broadcast_to(v, (8, 256))


def chain_back(maps, order, place):
    lam = order[3, 0:1, :]
    picked = jnp.where(place == 2, lam, 0.0)
    for j in (2, 1):
        lam = vec_mat(lam, maps[j]) + order[j, 0:1, :]
        picked = jnp.where(place == j - 1, lam, picked)
    return picked


def eye():
    r = lax.broadcasted_iota(jnp.int32, (256, 256), 0)
    c = lax.broadcasted_iota(jnp.int32, (256, 256), 1)
    return jnp.where(r == c, 1.0, 0.0).astype(F32)


def compose_body(ready, idx_ref, gx_ref, cx_ref, pz_ref, cz_ref, rest_z_ref, rest_ref, base_ref, until_z_ref, until_ref):
    x = idx_ref[1]
    z = idx_ref[2]

    def behind(maps, place):
        r = jnp.where(place < 3, maps[3], eye())
        r = jnp.where(place < 2, mat_mul(r, maps[2]), r)
        return jnp.where(place < 1, mat_mul(r, maps[1]), r)

    def ahead(maps, place):
        r = jnp.where(place > 0, maps[0], eye())
        r = jnp.where(place > 1, mat_mul(maps[1], r), r)
        return jnp.where(place > 2, mat_mul(maps[2], r), r)

    rest_z_ref[...] = behind(pz_ref, z)
    rest_ref[...] = mat_mul(behind(gx_ref, x), rest_z_ref[...])
    until_z_ref[...] = ahead(pz_ref, z)
    until_ref[...] = mat_mul(until_z_ref[...], ahead(gx_ref, x))
    lam = vec_mat(chain_back(gx_ref, cx_ref, x), rest_z_ref[...]) + chain_back(pz_ref, cz_ref, z)
    base_ref[...] = jnp.broadcast_to(lam, (8, 256))


def costate_body(
    ready, idx_ref, h0_ref, hm_ref, hp_ref, h2_ref,
    rest_z_ref, rest_ref, const_ref, w_ref, s0_ref, stat_ref,
    lam_ref, msg_ref, hy_ref, order_ref,
):
    y = idx_ref[0]
    x = idx_ref[1]
    refs = (h0_ref, hm_ref, hp_ref, h2_ref)
    order(hy_ref, y, *[r[0:256, :] for r in refs])
    order(order_ref, y, *[r[256:264, :] for r in refs])
    lam = vec_mat(chain_back(hy_ref, order_ref, y), rest_ref[...]) + const_ref[0:1, :]
    u1 = s0_ref[0:1, :] - vec_mat(lam, w_ref[...])
    u2 = vec_mat(u1, rest_z_ref[...], 1)
    u3 = vec_mat(u1, rest_ref[...], 1)
    d = lax.broadcasted_iota(jnp.int32, (64, 256), 0)
    group = lax.shift_right_logical(d, 2)
    plane = lax.shift_right_logical(d, 4)
    msg_ref[:, 0, 0:256] = jnp.where(group == y * 4 + x, u1, jnp.where(plane == y, u2, u3))
    msg_ref[:, 0, 256:384] = jnp.broadcast_to(stat_ref[0:1, :], (64, 128))
    lam_ref[...] = jnp.broadcast_to(lam, (8, 256))


def sweep_body(
    ready, quad_ref, a_ref, m_ref, g_ref, b_ref, src_ref, gi_ref, defect_ref, lam_ref,
    before_ref, gain_ref, base_ref, push_ref, entry_ref, after_ref,
):
    ready(0)
    backward_part(
        a_ref, m_ref, g_ref, quad_ref, b_ref, src_ref, gi_ref, lam_ref[0:1, :],
        before_ref, gain_ref, base_ref, push_ref, after_ref, lambda: ready(1),
    )
    ends = local_ends(a_ref, push_ref, defect_ref)
    entry_ref[...] = jnp.zeros_like(entry_ref)
    e = ends[0]
    for j in (1, 2, 3):
        entry_ref[j:j + 1, :] = e
        if j < 3:
            e = vec_mat(e, quad_ref[j], 1) + ends[j]


def chain_forth(maps, sums, place):
    e = sums[0]
    picked = jnp.where(place == 1, e, 0.0)
    for j in (1, 2):
        e = vec_mat(e, maps(j), 1) + sums[j]
        picked = jnp.where(place == j + 1, e, picked)
    return picked


def finish_body(
    ready, idx_ref,
    h0_ref, hm_ref, hp_ref, h2_ref, gx_ref, pz_ref, until_z_ref, until_ref, quad_ref, half_ref, third_ref,
    a_ref, v_ref, k_ref,
    active_ref, ub_ref, u_ref, iw_ref, defect_ref, before_ref, gain_ref, base_ref, push_ref, entry_ref,
    msg_ref,
    ss_ref, is_ref, ms_ref, bs_ref, norm_ref,
    hy_ref,
    *, horizon,
):
    y = idx_ref[0]
    x = idx_ref[1]
    z = idx_ref[2]
    d = lax.broadcasted_iota(jnp.int32, (64, 256), 0)
    plane = lax.shift_right_logical(d, 4)
    group = lax.shift_right_logical(d, 2)
    msg = msg_ref[:, 0, 0:256]

    def picked(mask):
        return jnp.sum(jnp.where(mask, msg, 0.0), axis=0, keepdims=True)

    ready(0)
    order(hy_ref, y, *[r[0:256, :] for r in (h0_ref, hm_ref, hp_ref, h2_ref)])
    ey = chain_forth(lambda j: hy_ref[j], [picked(plane == j) for j in range(3)], y)
    ex = chain_forth(lambda j: gx_ref[j - 1], [picked(group == y * 4 + j) for j in range(3)], x)
    ez = chain_forth(lambda j: pz_ref[j - 1], [picked(d == y * 16 + x * 4 + j) for j in range(3)], z)
    e = vec_mat(ey, until_ref[...], 1) + vec_mat(ex, until_z_ref[...], 1) + ez
    sums = jnp.sum(msg_ref[:, 0, 256:384], axis=0, keepdims=True)
    lane = lax.broadcasted_iota(jnp.int32, (1, 128), 1)
    share = floor_share * horizon
    floors = jnp.where(lane == 0, share * 256, jnp.where(lane == 1, share * 320, share * 64))
    norm_ref[...] = jnp.sqrt(sums / (pltpu.roll(sums, 125, 1) + floors))[:, 0:3]

    entries = [e] + [
        vec_mat(e, m, 1) + entry_ref[j:j + 1, :]
        for j, m in ((1, quad_ref[0]), (2, half_ref[...]), (3, third_ref[...]))
    ]
    ready(1)
    for m in range(4):
        for j in range(4):
            k = 4 * j + m
            step = entries[j] - defect_ref[k:k + 1, :]
            ss_ref[k:k + 1, :] = step
            if m < 3:
                entries[j] = vec_mat(step, a_ref[k], 1) + push_ref[k:k + 1, :]
    ready(2)
    for k in range(16):
        step = ss_ref[k:k + 1, :]
        ms_ref[k:k + 1, :] = vec_mat(step - defect_ref[k:k + 1, :], v_ref[k]) + before_ref[k:k + 1, :]
        is_ref[k:k + 1, :] = vec_mat(step, k_ref[k], 1) + gain_ref[k:k + 1, :]
    chosen = active_ref[...].astype(F32)
    step = (1.0 - chosen) * is_ref[...] + chosen * (ub_ref[...] - u_ref[...])
    is_ref[...] = step
    bs_ref[...] = chosen * (base_ref[...] + mat_mul(step, iw_ref[...], 1, 1))


def sds(*shape):
    return jax.ShapeDtypeStruct(shape, F32)


SCALARS = pl.BlockSpec(memory_space=SMEM)
FULL = pl.BlockSpec(memory_space=VMEM)


def in_vmem(shape):
    return pltpu.VMEM(shape, F32)


def part(array, slot=0, chunks=1, low=0, size=None):
    return array, slot, chunks, low, array.shape[0] if size is None else size


def call(body, scalars, big, small, near, outs, scratch, final=False, away=()):
    ns, nn, no = len(scalars), len(near), len(outs)
    far = list(big) + [part(a, -1) for a in small]
    slots = max([p[1] + p[2] for p in far] + [0])

    def kernel(*refs):
        refs = list(refs)

        def take(n):
            out = refs[:n]
            del refs[:n]
            return out

        scalar_refs, far_refs, near_refs, out_refs, local_refs = take(ns), take(len(far)), take(nn), take(no), take(len(far))
        sems = refs.pop() if far else None
        moves = [[] for _ in range(slots)]
        first = []
        n = 0
        for (_, slot, chunks, low, size), src, dst in zip(far, far_refs, local_refs):
            step = size // chunks
            for c in range(chunks):
                move = pltpu.make_async_copy(
                    src.at[pl.ds(low + c * step, step)], dst.at[pl.ds(c * step, step)], sems.at[n]
                )
                (first if slot < 0 else moves[slot + c]).append(move)
                n += 1
        for group in [first] + moves:
            for move in group:
                move.start()
        for move in first:
            move.wait()

        def ready(c):
            for move in moves[c]:
                move.wait()

        body(ready, *scalar_refs, *local_refs, *near_refs, *out_refs, *refs)

    rooms = [pltpu.VMEM((p[4],) + p[0].shape[1:], p[0].dtype) for p in far]
    sems = [pltpu.SemaphoreType.DMA((sum(p[2] for p in far),))] if far else []
    return pl.pallas_call(
        kernel,
        in_specs=[SCALARS] * ns + [pl.BlockSpec(memory_space=pltpu.HBM)] * len(far) + [FULL] * nn,
        out_specs=[FULL] * no,
        out_shape=[sds(*o) if final else (pltpu.HBM(o, F32) if n in away else in_vmem(o)) for n, o in enumerate(outs)],
        scratch_shapes=rooms + scratch + sems,
        compiler_params=pltpu.CompilerParams(vmem_limit_bytes=24 * 1024 * 1024),
    )(*scalars, *[pltpu.with_memory_space_constraint(p[0], pltpu.HBM) for p in far], *near)


def room(*shape):
    return VMEM(shape, F32)


def turned(x, axis):
    def move(by):
        return lax.ppermute(x, axis, [(i, (i + by) % 4) for i in range(4)])

    return move(1), move(-1), move(2)


def shifted(x, by):
    pairs = [(i, i + by) for i in range(64) if 0 <= i + by < 64]
    return lax.ppermute(x, TM, pairs)


def local(
    state_map,
    input_map,
    closed_loop,
    feedback,
    value_matrix,
    gain_inverse,
    input_weight,
    state_weight,
    state_linear,
    input_linear,
    offset,
    upper_bound,
    states,
    inputs,
    multipliers,
    bound_mult,
    active,
):
    place = jnp.stack([lax.axis_index(a) for a in TM]).astype(jnp.int32)

    place, ahead = lax.optimization_barrier((place, multipliers[:8]))
    from_after = shifted(ahead, -1)
    (last,) = call(
        last_prediction_body, [],
        [part(state_map, 0, 1, 15, 1), part(input_map, 0, 1, 15, 1), part(states, 0, 1, 8, 8), part(inputs, 0, 1, 8, 8)],
        [], [], [(8, 256)], [],
    )
    from_before = shifted(last, 1)

    loops, last = lax.optimization_barrier((closed_loop, last))
    sections = [loops, state_map, input_map, value_matrix, feedback, gain_inverse]
    rows = [
        states, inputs, multipliers, bound_mult, upper_bound, offset, state_weight, state_linear, input_linear,
        input_weight,
    ]
    kept = sections + rows
    out = pl.pallas_call(
        functools.partial(block_product_body, sections=sections, rows=len(rows)),
        in_specs=[pl.BlockSpec(memory_space=pltpu.HBM)] * len(kept),
        out_specs=[FULL] * (4 + len(kept)),
        out_shape=[in_vmem(o) for o in [(256, 256), (4, 256, 256), (4, 256, 256), (256, 256)] + [k.shape for k in kept]],
        scratch_shapes=[room(4, 256, 256), pltpu.SemaphoreType.DMA((3 + len(kept),))],
        compiler_params=pltpu.CompilerParams(vmem_limit_bytes=24 * 1024 * 1024),
        name="block_product",
    )(*[pltpu.with_memory_space_constraint(k, pltpu.HBM) for k in kept])
    product, pairs, quads, half = out[:4]
    loop_v, map_v, push_v, value_v, feed_v, inverse_v = out[4:10]
    rows_v = out[10:]

    defect, grad_input, sources, inner, block, statistics = call(
        sources_body, [],
        [], [],
        [map_v, push_v, value_v, feed_v, loop_v, *rows_v, quads, half, product, from_before, from_after],
        [(16, 256), (16, 64), (16, 256), (16, 256), (264, 256), (8, 128)],
        [room(16, 256)],
    )
    near_z = turned(block, "tm_2")

    def join(axis, *parts):
        return call(
            functools.partial(join_body, axis=axis), [place], [], [],
            list(parts),
            [(4, 256, 256), (4, 8, 256), (264, 256)], [],
        )

    pairs, block = lax.optimization_barrier((pairs, block))
    weight, third = call(
        weight_body, [], [], [], [loop_v, push_v, inverse_v, pairs, quads, half],
        [(256, 256), (256, 256)], [room(1024, 256), room(1024, 256)],
    )
    near_z, weight, third = lax.optimization_barrier((near_z, weight, third))
    maps_z, vectors_z, group = join(2, block, *near_z)
    near_x = turned(group, "tm_1")

    inner, group = lax.optimization_barrier((inner, group))
    (local_state,) = call(
        local_body, [], [], [],
        [loop_v, push_v, inverse_v, quads, inner, sources, grad_input, defect],
        [(8, 256)],
        [room(16, 256), room(16, 64), room(16, 64), room(16, 256), room(16, 256)],
    )
    near_x, local_state = lax.optimization_barrier((near_x, local_state))
    maps_x, vectors_x, plane = join(1, group, *near_x)
    near_y = turned(plane, "tm_0")

    maps_x, plane = lax.optimization_barrier((maps_x, plane))
    rest_z, rest, constant, until_z, until = call(
        compose_body, [place], [], [], [maps_x, vectors_x, maps_z, vectors_z],
        [(256, 256), (256, 256), (8, 256), (256, 256), (256, 256)], [],
    )

    incoming, message = call(
        costate_body, [place], [], [],
        [plane, *near_y, rest_z, rest, constant, weight, local_state, statistics],
        [(8, 256), (64, 1, 384)], [room(4, 256, 256), room(4, 8, 256)], away=(0, 1),
    )

    received = lax.all_to_all(message, TM, 0, 0, tiled=True)

    before, gain, base, push, entry = call(
        sweep_body, [], [part(quads), part(closed_loop, 1), part(input_map, 1), part(gain_inverse, 1)],
        [inner, sources, grad_input, defect, incoming], [],
        [(16, 256), (16, 64), (16, 64), (16, 256), (8, 256)], [room(16, 256)], away=range(5),
    )

    state_step, input_step, multiplier_step, bound_step, sums = call(
        functools.partial(finish_body, horizon=states.shape[0] * lax.axis_size(TM)), [place],
        [part(a) for a in (plane, *near_y)]
        + [part(a, 0, 1, 1, 2) for a in (maps_x, maps_z)]
        + [part(until_z), part(until), part(quads, 0, 1, 0, 1), part(half), part(third)]
        + [part(closed_loop, 1), part(value_matrix, 2), part(feedback, 2)],
        [active, upper_bound, inputs, input_weight, defect, before, gain, base, push, entry],
        [received],
        [(16, 256), (16, 64), (16, 256), (16, 64), (1, 3)],
        [room(4, 256, 256)], final=True,
    )

    kkt_norms = sums.reshape(3)
    return (state_step, input_step, multiplier_step, bound_step, kkt_norms)


def solution(mesh):
    split = Mesh(
        mesh.devices.reshape(4, 4, 4, mesh.shape["batch"]), ("tm_0", "tm_1", "tm_2", "batch")
    )

    return jax.shard_map(
        local,
        mesh=split,
        in_specs=(P(BATCH_TM, None, None),) * 6 + (P("batch", None),) + (P(BATCH_TM, None),) * 10,
        out_specs=(P(BATCH_TM, None),) * 4 + (P("batch"),),
        check_vma=False,
    )
```

time: 111 us -> 104 us (0.937)
  waiting for transfers between devices: 11.9 us -> 21.4 us
  Pallas kernels: 53.1 us -> 44.8 us
  local copies, waits for them, and re-layouts: 8.38 us -> 2.17 us
  starting transfers between devices: 36.3 us -> 34.1 us
    ppermute x12 -> x9, waiting for transfers between devices: 5.8 us -> 19.9 us  [move(): return lax.ppermute(x, axis, [(i, (i + by) % 4) for i in range(4)])]
    pallas_call x10, Pallas kernels: 53.1 us -> 39.3 us  [call(): pl.pallas_call(kernel, in_specs=[SCALARS] * ns + [pl.BlockSpec(memory_spa...]
    unnamed x44 -> x30, local copies, waits for them, and re-layouts: 8.38 us -> 1.47 us
    pallas_call x0 -> x1, Pallas kernels: none -> 5.55 us  [local(): pl.pallas_call(functools.partial(block_product_body, sections=sections, r...]
    ppermute x12 -> x9, starting transfers between devices: 24.8 us -> 19.7 us  [move(): return lax.ppermute(x, axis, [(i, (i + by) % 4) for i in range(4)])]
    ppermute x2, waiting for transfers between devices: 4.92 us -> 0.01 us  [shifted(): return lax.ppermute(x, TM, pairs)]
    all_to_all x1, starting transfers between devices: 5.64 us -> 8.59 us  [local(): received = lax.all_to_all(message, TM, 0, 0, tiled=True)]
  transfers between devices with their start and end apart: 15 -> 12, of which waited for: 6 -> 5; matrix products, arithmetic and copies ran while one was open for 0% -> 0% of each run, Pallas kernels for 28% -> 26%
where the time goes in v2:
time: 104 us
  Pallas kernels  44.8 us (43%)
  starting transfers between devices  34.1 us (33%)
  waiting for transfers between devices  21.4 us (21%)
  local copies, waits for them, and re-layouts  2.17 us (2%)
  between operations  1.1 us (1%)
    pallas_call x10, Pallas kernels, call(): pl.pallas_call(kernel, in_specs=[SCALARS] * ns + [pl.BlockSpec(memory_spa...  39.3 us
    ppermute x9, waiting for transfers between devices, move(): return lax.ppermute(x, axis, [(i, (i + by) % 4) for i in range(4)])  19.9 us
    ppermute x9, starting transfers between devices, move(): return lax.ppermute(x, axis, [(i, (i + by) % 4) for i in range(4)])  19.7 us
    all_to_all x1, starting transfers between devices, local(): received = lax.all_to_all(message, TM, 0, 0, tiled=True)  8.59 us
    ppermute x2, starting transfers between devices, shifted(): return lax.ppermute(x, TM, pairs)  5.84 us
    pallas_call x1, Pallas kernels, local(): pl.pallas_call(functools.partial(block_product_body, sections=sections, r...  5.55 us
  transfers between devices with their start and end apart: 12, of which 5 were waited for; matrix products, arithmetic and copies ran while one was open for 0% of the time, Pallas kernels for 26%

profile of v2, /device:TPU:0, one launch (start us, length us, event | category | flops | bytes accessed | tf_op | source)
XLA Modules:
  0.0 103.6 jit_solution(5004487578150915907)
XLA Ops:
  0.6 0.7 slice.3
  1.3 0.1 pad_add_fusion.refs_0_
  1.4 1.3 %collective-permute-start.1 = (f32[8,256]{1,0:T(8,128)S(1)}, f32[8,256]{1,0:T(8,128)S(1)}, u32[]{:S(2)}, u32[]{:S(2)}) collective-permute-start(f32[8,256]{1,0:T(8,128)S(1)} %slice.3), channel_id=1, source_target_pairs={{2,0},{4,2},{6,4},{8,6},{10,8},{12,10},{14,12},{16,14},{18,16},{20... | collective-permute-start | bytes 24584 | tf_op jit(solution)/shard_map/ppermute | solution.py:452
  2.7 1.2 %shard_map.200 = f32[8,256]{1,0:T(8,128)S(1)} custom-call(f32[16,256,256]{2,1,0:T(8,128)} %refs_1_.4, f32[16,64,256]{2,1,0:T(8,128)} %refs_2_.5, f32[16,256]{1,0:T(8,128)} %refs_6_.1, f32[16,64]{1,0:T(8,128)} %refs_17_.1), custom_call_target="tpu_custom_call" | custom-call | tf_op jit(solution)/shard_map/pallas_call | solution.py:429
  3.9 4.6 %collective-permute-start = (f32[8,256]{1,0:T(8,128)S(1)}, f32[8,256]{1,0:T(8,128)S(1)}, u32[]{:S(2)}, u32[]{:S(2)}) collective-permute-start(f32[8,256]{1,0:T(8,128)S(1)} %shard_map.200), channel_id=1, source_target_pairs={{0,2},{2,4},{4,6},{6,8},{8,10},{10,12},{12,14},{14,16},{16,18},{18... | collective-permute-start | bytes 24584 | tf_op jit(solution)/shard_map/ppermute | solution.py:452
  8.5 5.5 %block_product.1 = (f32[256,256]{1,0:T(8,128)S(1)}, f32[4,256,256]{2,1,0:T(8,128)S(1)}, f32[4,256,256]{2,1,0:T(8,128)S(1)}, f32[256,256]{1,0:T(8,128)S(1)}, f32[...) custom-call(f32[16,256,256]{2,1,0:T(8,128)} %refs_12_.3, ...), custom_call_target="tpu_custom_call" | custom-call | tf_op jit(solution)/shard_map/block_product/pallas_call | solution.py:492
  14.1 0.0 collective-permute-done.1.refs_19_
  14.1 0.0 collective-permute-done.refs_18_
  14.1 5.5 %shard_map.201 = (f32[16,256]{1,0:T(8,128)S(1)}, f32[16,64]{1,0:T(8,128)S(1)}, f32[16,256]{1,0:T(8,128)S(1)}, f32[16,256]{1,0:T(8,128)S(1)}, f32[264,256]{1,0:T(8,128)S(1)}, /*index=5*/f32[8,128]{1,0:T(8,128)S(1)}) custom-call(f32[16,256,256]{2,1,0:T(8,128)S(1)} %get-tuple-element.76.refs_0_, f32[16,64,256]{2,1,0:T(8,128)S(1)} %get-tuple-element.77.refs_1_, ...), custom_call_target="tpu_custom_call" | custom-call | tf_op jit(solution)/shard_map/pallas_call | solution.py:429
  19.6 0.0 copy-start.11
  19.6 0.0 copy-start.12
  19.6 0.0 copy-start.13
  19.6 0.0 copy-start.14
  19.6 4.1 %collective-permute-start.4 = (f32[264,256]{1,0:T(8,128)S(1)}, f32[264,256]{1,0:T(8,128)S(1)}, u32[]{:S(2)}, u32[]{:S(2)}) collective-permute-start(f32[264,256]{1,0:T(8,128)S(1)} %get-tuple-element.98.refs_1_), channel_id=1, source_target_pairs={{0,4},{2,6},{4,0},{6,2},{1,5},{3,7},{5,1},{7,3},{8,12},{10,14},{12... | collective-permute-start | bytes 811016 | tf_op jit(solution)/shard_map/ppermute | solution.py:445
  23.7 2.4 %collective-permute-start.3 = (f32[264,256]{1,0:T(8,128)S(1)}, f32[264,256]{1,0:T(8,128)S(1)}, u32[]{:S(2)}, u32[]{:S(2)}) collective-permute-start(f32[264,256]{1,0:T(8,128)S(1)} %get-tuple-element.98.refs_1_), channel_id=1, source_target_pairs={{0,6},{2,0},{4,2},{6,4},{1,7},{3,1},{5,3},{7,5},{8,14},{10,8},{12,... | collective-permute-start | bytes 811016 | tf_op jit(solution)/shard_map/ppermute | solution.py:445
  26.0 0.8 collective-permute-start.2
  26.8 4.2 %shard_map.202 = (f32[256,256]{1,0:T(8,128)S(1)}, f32[256,256]{1,0:T(8,128)S(1)}) custom-call(f32[16,256,256]{2,1,0:T(8,128)S(1)} %get-tuple-element.80.refs_4_.refs_0_, f32[16,64,256]{2,1,0:T(8,128)S(1)} %get-tuple-element.77.refs_1_, f32[16,64,64]{2,1,0:T(8,128)S(1)} %get-tuple-element.99.refs_2_, f32[4,256,256]{2,1,0:T(8,128)S(1)} %get-tuple-element.100.refs_3_, ...), custom_call_target="tpu_custom_call" | custom-call | tf_op jit(solution)/shard_map/pallas_call | solution.py:429
  31.0 0.0 collective-permute-done.4.refs_4_
  31.1 7.2 %collective-permute-done.3.refs_3_ = f32[264,256]{1,0:T(8,128)S(1)} collective-permute-done((f32[264,256]{1,0:T(8,128)S(1)}, f32[264,256]{1,0:T(8,128)S(1)}, u32[]{:S(2)}, u32[]{:S(2)}) %collective-permute-start.3) | collective-permute-done | bytes 270368 | tf_op jit(solution)/shard_map/ppermute | solution.py:445
  38.3 0.0 collective-permute-done.2.refs_2_
  38.3 1.6 %shard_map.203 = (f32[4,256,256]{2,1,0:T(8,128)S(1)}, f32[4,8,256]{2,1,0:T(8,128)S(1)}, f32[264,256]{1,0:T(8,128)S(1)}) custom-call(s32[3]{0:T(128)S(1)} %pad_add_fusion.refs_0_, f32[264,256]{1,0:T(8,128)S(1)} %get-tuple-element.98.refs_1_, f32[264,256]{1,0:T(8,128)S(1)} %collective-permute-done.2.refs_2_, f32[264,256]{1,0:T(8,128)S(1)} %collective-permute-done.3.refs_3_, ...), custom_call_target="tpu_custom_call" | custom-call | tf_op jit(solution)/shard_map/pallas_call | solution.py:429
  39.9 3.3 %collective-permute-start.7 = (f32[264,256]{1,0:T(8,128)S(1)}, f32[264,256]{1,0:T(8,128)S(1)}, u32[]{:S(2)}, u32[]{:S(2)}) collective-permute-start(f32[264,256]{1,0:T(8,128)S(1)} %get-tuple-element.107.refs_1_), channel_id=1, source_target_pairs={{0,16},{8,24},{16,0},{24,8},{1,17},{9,25},{17,1},{25,9},{2,18},{10... | collective-permute-start | bytes 811016 | tf_op jit(solution)/shard_map/ppermute | solution.py:445
  43.1 1.9 %collective-permute-start.6 = (f32[264,256]{1,0:T(8,128)S(1)}, f32[264,256]{1,0:T(8,128)S(1)}, u32[]{:S(2)}, u32[]{:S(2)}) collective-permute-start(f32[264,256]{1,0:T(8,128)S(1)} %get-tuple-element.107.refs_1_), channel_id=1, source_target_pairs={{0,24},{8,0},{16,8},{24,16},{1,25},{9,1},{17,9},{25,17},{2,26},{10... | collective-permute-start | bytes 811016 | tf_op jit(solution)/shard_map/ppermute | solution.py:445
  45.1 0.8 collective-permute-start.5
  45.8 0.0 copy-done.11
  45.9 5.1 %shard_map.204.refs_9_ = f32[8,256]{1,0:T(8,128)S(1)} custom-call(f32[16,256,256]{2,1,0:T(8,128)S(1)} %get-tuple-element.80.refs_4_.refs_0_, f32[16,64,256]{2,1,0:T(8,128)S(1)} %get-tuple-element.77.refs_1_, f32[16,64,64]{2,1,0:T(8,128)S(1)} %get-tuple-element.99.refs_2_, f32[4,256,256]{2,1,0:T(8,128)S(1)} %get-tuple-element.91.refs_15_.refs_4_.refs_3_.refs_0_.refs_9_, ...), custom_call_target="tpu_custom_call" | custom-call | tf_op jit(solution)/shard_map/pallas_call | solution.py:429
  50.9 0.0 collective-permute-done.7.refs_4_
  51.0 5.6 %collective-permute-done.6.refs_3_ = f32[264,256]{1,0:T(8,128)S(1)} collective-permute-done((f32[264,256]{1,0:T(8,128)S(1)}, f32[264,256]{1,0:T(8,128)S(1)}, u32[]{:S(2)}, u32[]{:S(2)}) %collective-permute-start.6) | collective-permute-done | bytes 270368 | tf_op jit(solution)/shard_map/ppermute | solution.py:445
  56.6 0.0 collective-permute-done.5.refs_2_
  56.6 1.6 %shard_map.205 = (f32[4,256,256]{2,1,0:T(8,128)S(1)}, f32[4,8,256]{2,1,0:T(8,128)S(1)}, f32[264,256]{1,0:T(8,128)S(1)}) custom-call(s32[3]{0:T(128)S(1)} %pad_add_fusion.refs_0_, f32[264,256]{1,0:T(8,128)S(1)} %get-tuple-element.107.refs_1_, f32[264,256]{1,0:T(8,128)S(1)} %collective-permute-done.5.refs_2_, f32[264,256]{1,0:T(8,128)S(1)} %collective-permute-done.6.refs_3_, ...), custom_call_target="tpu_custom_call" | custom-call | tf_op jit(solution)/shard_map/pallas_call | solution.py:429
  58.2 4.5 %collective-permute-start.10 = (f32[264,256]{1,0:T(8,128)S(1)}, f32[264,256]{1,0:T(8,128)S(1)}, u32[]{:S(2)}, u32[]{:S(2)}) collective-permute-start(f32[264,256]{1,0:T(8,128)S(1)} %get-tuple-element.117.refs_1_), channel_id=1, source_target_pairs={{0,64},{32,96},{64,0},{96,32},{1,65},{33,97},{65,1},{97,33},{2,66}... | collective-permute-start | bytes 811016 | tf_op jit(solution)/shard_map/ppermute | solution.py:445
  62.6 1.1 %collective-permute-start.9 = (f32[264,256]{1,0:T(8,128)S(1)}, f32[264,256]{1,0:T(8,128)S(1)}, u32[]{:S(2)}, u32[]{:S(2)}) collective-permute-start(f32[264,256]{1,0:T(8,128)S(1)} %get-tuple-element.117.refs_1_), channel_id=1, source_target_pairs={{0,96},{32,0},{64,32},{96,64},{1,97},{33,1},{65,33},{97,65},{2,98}... | collective-permute-start | bytes 811016 | tf_op jit(solution)/shard_map/ppermute | solution.py:445
  63.7 1.0 collective-permute-start.8
  64.6 2.7 %shard_map.206 = (f32[256,256]{1,0:T(8,128)S(1)}, f32[256,256]{1,0:T(8,128)S(1)}, f32[8,256]{1,0:T(8,128)S(1)}, f32[256,256]{1,0:T(8,128)S(1)}, f32[256,256]{1,0:T(8,128)S(1)}) custom-call(s32[3]{0:T(128)S(1)} %pad_add_fusion.refs_0_, f32[4,256,256]{2,1,0:T(8,128)S(1)} %get-tuple-element.118.refs_1_.refs_5_, f32[4,8,256]{2,1,0:T(8,128)S(1)} %get-tuple-element.120.refs_2_, ...), custom_call_target="tpu_custom_call" | custom-call | tf_op jit(solution)/shard_map/pallas_call | solution.py:429
  67.4 0.7 copy-done.9
  68.1 0.7 copy-done.10
  68.8 1.2 %collective-permute-done.10.refs_4_ = f32[264,256]{1,0:T(8,128)S(1)} collective-permute-done((f32[264,256]{1,0:T(8,128)S(1)}, f32[264,256]{1,0:T(8,128)S(1)}, u32[]{:S(2)}, u32[]{:S(2)}) %collective-permute-start.10) | collective-permute-done | bytes 270368 | tf_op jit(solution)/shard_map/ppermute | solution.py:445
  70.0 5.8 %collective-permute-done.9.refs_3_ = f32[264,256]{1,0:T(8,128)S(1)} collective-permute-done((f32[264,256]{1,0:T(8,128)S(1)}, f32[264,256]{1,0:T(8,128)S(1)}, u32[]{:S(2)}, u32[]{:S(2)}) %collective-permute-start.9) | collective-permute-done | bytes 270368 | tf_op jit(solution)/shard_map/ppermute | solution.py:445
  75.8 0.0 collective-permute-done.8.refs_2_
  75.8 2.3 %shard_map.207 = (f32[8,256]{1,0:T(8,128)}, f32[64,1,384]{2,1,0:T(1,128)}) custom-call(s32[3]{0:T(128)S(1)} %pad_add_fusion.refs_0_, f32[264,256]{1,0:T(8,128)S(1)} %get-tuple-element.117.refs_1_, f32[264,256]{1,0:T(8,128)S(1)} %collective-permute-done.8.refs_2_, f32[264,256]{1,0:T(8,128)S(1)} %collective-permute-done.9.refs_3_, ...), custom_call_target="tpu_custom_call" | custom-call | tf_op jit(solution)/shard_map/pallas_call | solution.py:429
  78.1 8.6 %all-to-all-start = ((f32[64,1,384]{2,1,0:T(1,128)}), f32[64,1,384]{2,1,0:T(1,128)S(1)}, u32[]{:S(2)}, u32[]{:S(2)}) async-start(f32[64,1,384]{2,1,0:T(1,128)} %get-tuple-element.137), calls=%async_computation | async-start | bytes 196608 | tf_op jit(solution)/shard_map/all_to_all | solution.py:553
  86.7 8.0 %shard_map.208 = (f32[16,256]{1,0:T(8,128)}, f32[16,64]{1,0:T(8,128)}, f32[16,64]{1,0:T(8,128)}, f32[16,256]{1,0:T(8,128)}, f32[8,256]{1,0:T(8,128)}) custom-call(f32[4,256,256]{2,1,0:T(8,128)} %copy-done, f32[16,256,256]{2,1,0:T(8,128)} %refs_12_.3, f32[16,64,256]{2,1,0:T(8,128)} %refs_2_.5, f32[16,64,64]{2,1,0:T(8,128)} %refs_3_.5, f32[16,256]{1,0:T(8,128)} %copy-done.13, ...), custom_call_target="tpu_custom_call" | custom-call | tf_op jit(solution)/shard_map/pallas_call | solution.py:429
  94.7 0.0 copy-done.2
  94.7 0.0 copy-done.4
  94.7 0.0 copy-done.5
  94.7 0.0 copy-done.6
  94.7 1.5 %all-to-all-done.refs_25_ = f32[64,1,384]{2,1,0:T(1,128)S(1)} async-done(((f32[64,1,384]{2,1,0:T(1,128)}), f32[64,1,384]{2,1,0:T(1,128)S(1)}, u32[]{:S(2)}, u32[]{:S(2)}) %all-to-all-start) | async-done | bytes 98336 | tf_op jit(solution)/shard_map/all_to_all | solution.py:553
  96.2 7.3 %shard_map.209 = (f32[16,256]{1,0:T(8,128)}, f32[16,64]{1,0:T(8,128)}, f32[16,256]{1,0:T(8,128)}, f32[16,64]{1,0:T(8,128)}, f32[1,3]{1,0:T(1,128)}) custom-call(s32[3]{0:T(128)S(1)} %pad_add_fusion.refs_0_, f32[264,256]{1,0:T(8,128)} %copy-done.4, f32[264,256]{1,0:T(8,128)} %copy-done.7, f32[264,256]{1,0:T(8,128)} %copy-done.6, f32[264,256]{1,0:T(8,128)} %copy-done.5, ...), custom_call_target="tpu_custom_call" | custom-call | tf_op jit(solution)/shard_map/pallas_call | solution.py:429
  (19 shorter events, 0.0 us)
Async XLA Ops:
  1.4 12.6 %collective-permute-start.1 = (f32[8,256]{1,0:T(8,128)S(1)}, f32[8,256]{1,0:T(8,128)S(1)}, u32[]{:S(2)}, u32[]{:S(2)}) collective-permute-start(f32[8,256]{1,0:T(8,128)S(1)} %slice.3), channel_id=1, source_target_pairs={{2,0},{4,2},{6,4},{8,6},{10,8},{12,10},{14,12},{16,14},{18,16},{20... | collective-permute-start | bytes 24584 | tf_op jit(solution)/shard_map/ppermute | solution.py:452
  3.9 10.2 %collective-permute-start = (f32[8,256]{1,0:T(8,128)S(1)}, f32[8,256]{1,0:T(8,128)S(1)}, u32[]{:S(2)}, u32[]{:S(2)}) collective-permute-start(f32[8,256]{1,0:T(8,128)S(1)} %shard_map.200), channel_id=1, source_target_pairs={{0,2},{2,4},{4,6},{6,8},{8,10},{10,12},{12,14},{14,16},{16,18},{18... | collective-permute-start | bytes 24584 | tf_op jit(solution)/shard_map/ppermute | solution.py:452
  14.0 12.8 %copy-start.3 = (f32[256,256]{1,0:T(8,128)}, f32[256,256]{1,0:T(8,128)S(1)}, u32[]{:S(2)}) copy-start(f32[256,256]{1,0:T(8,128)S(1)} %get-tuple-element.92.refs_16_.refs_5_.refs_10_) | copy-start | bytes 786436
  14.0 31.8 %copy-start = (f32[4,256,256]{2,1,0:T(8,128)}, f32[4,256,256]{2,1,0:T(8,128)S(1)}, u32[]{:S(2)}) copy-start(f32[4,256,256]{2,1,0:T(8,128)S(1)} %get-tuple-element.91.refs_15_.refs_4_.refs_3_.refs_0_.refs_9_) | copy-start | bytes 3145732
  19.6 26.3 %copy-start.11 = (f32[16,256]{1,0:T(8,128)}, f32[16,256]{1,0:T(8,128)S(1)}, u32[]{:S(2)}) copy-start(f32[16,256]{1,0:T(8,128)S(1)} %get-tuple-element.111.refs_7_.refs_19_) | copy-start | bytes 49156
  19.6 26.3 %copy-start.12 = (f32[16,256]{1,0:T(8,128)}, f32[16,256]{1,0:T(8,128)S(1)}, u32[]{:S(2)}) copy-start(f32[16,256]{1,0:T(8,128)S(1)} %get-tuple-element.109.refs_5_) | copy-start | bytes 49156
  19.6 26.3 %copy-start.13 = (f32[16,256]{1,0:T(8,128)}, f32[16,256]{1,0:T(8,128)S(1)}, u32[]{:S(2)}) copy-start(f32[16,256]{1,0:T(8,128)S(1)} %get-tuple-element.108.refs_4_) | copy-start | bytes 49156
  19.6 26.3 %copy-start.14 = (f32[16,64]{1,0:T(8,128)}, f32[16,64]{1,0:T(8,128)S(1)}, u32[]{:S(2)}) copy-start(f32[16,64]{1,0:T(8,128)S(1)} %get-tuple-element.110.refs_6_) | copy-start | bytes 12292
  19.6 11.4 %collective-permute-start.4 = (f32[264,256]{1,0:T(8,128)S(1)}, f32[264,256]{1,0:T(8,128)S(1)}, u32[]{:S(2)}, u32[]{:S(2)}) collective-permute-start(f32[264,256]{1,0:T(8,128)S(1)} %get-tuple-element.98.refs_1_), channel_id=1, source_target_pairs={{0,4},{2,6},{4,0},{6,2},{1,5},{3,7},{5,1},{7,3},{8,12},{10,14},{12... | collective-permute-start | bytes 811016 | tf_op jit(solution)/shard_map/ppermute | solution.py:445
  23.7 14.6 %collective-permute-start.3 = (f32[264,256]{1,0:T(8,128)S(1)}, f32[264,256]{1,0:T(8,128)S(1)}, u32[]{:S(2)}, u32[]{:S(2)}) collective-permute-start(f32[264,256]{1,0:T(8,128)S(1)} %get-tuple-element.98.refs_1_), channel_id=1, source_target_pairs={{0,6},{2,0},{4,2},{6,4},{1,7},{3,1},{5,3},{7,5},{8,14},{10,8},{12,... | collective-permute-start | bytes 811016 | tf_op jit(solution)/shard_map/ppermute | solution.py:445
  26.0 12.3 %collective-permute-start.2 = (f32[264,256]{1,0:T(8,128)S(1)}, f32[264,256]{1,0:T(8,128)S(1)}, u32[]{:S(2)}, u32[]{:S(2)}) collective-permute-start(f32[264,256]{1,0:T(8,128)S(1)} %get-tuple-element.98.refs_1_), channel_id=1, source_target_pairs={{0,2},{2,4},{4,6},{6,0},{1,3},{3,5},{5,7},{7,1},{8,10},{10,12},{12... | collective-permute-start | bytes 811016 | tf_op jit(solution)/shard_map/ppermute | solution.py:445
  31.0 8.8 %copy-start.8 = (f32[256,256]{1,0:T(8,128)}, f32[256,256]{1,0:T(8,128)S(1)}, u32[]{:S(2)}) copy-start(f32[256,256]{1,0:T(8,128)S(1)} %get-tuple-element.124.refs_11_) | copy-start | bytes 786436
  39.8 27.5 %copy-start.1 = (f32[4,256,256]{2,1,0:T(8,128)}, f32[4,256,256]{2,1,0:T(8,128)S(1)}, u32[]{:S(2)}) copy-start(f32[4,256,256]{2,1,0:T(8,128)S(1)} %get-tuple-element.119.refs_3_.refs_6_) | copy-start | bytes 3145732
  39.9 11.1 %collective-permute-start.7 = (f32[264,256]{1,0:T(8,128)S(1)}, f32[264,256]{1,0:T(8,128)S(1)}, u32[]{:S(2)}, u32[]{:S(2)}) collective-permute-start(f32[264,256]{1,0:T(8,128)S(1)} %get-tuple-element.107.refs_1_), channel_id=1, source_target_pairs={{0,16},{8,24},{16,0},{24,8},{1,17},{9,25},{17,1},{25,9},{2,18},{10... | collective-permute-start | bytes 811016 | tf_op jit(solution)/shard_map/ppermute | solution.py:445
  43.1 13.4 %collective-permute-start.6 = (f32[264,256]{1,0:T(8,128)S(1)}, f32[264,256]{1,0:T(8,128)S(1)}, u32[]{:S(2)}, u32[]{:S(2)}) collective-permute-start(f32[264,256]{1,0:T(8,128)S(1)} %get-tuple-element.107.refs_1_), channel_id=1, source_target_pairs={{0,24},{8,0},{16,8},{24,16},{1,25},{9,1},{17,9},{25,17},{2,26},{10... | collective-permute-start | bytes 811016 | tf_op jit(solution)/shard_map/ppermute | solution.py:445
  45.1 11.5 %collective-permute-start.5 = (f32[264,256]{1,0:T(8,128)S(1)}, f32[264,256]{1,0:T(8,128)S(1)}, u32[]{:S(2)}, u32[]{:S(2)}) collective-permute-start(f32[264,256]{1,0:T(8,128)S(1)} %get-tuple-element.107.refs_1_), channel_id=1, source_target_pairs={{0,8},{8,16},{16,24},{24,0},{1,9},{9,17},{17,25},{25,1},{2,10},{10... | collective-permute-start | bytes 811016 | tf_op jit(solution)/shard_map/ppermute | solution.py:445
  58.1 36.5 %copy-start.2 = (f32[4,256,256]{2,1,0:T(8,128)}, f32[4,256,256]{2,1,0:T(8,128)S(1)}, u32[]{:S(2)}) copy-start(f32[4,256,256]{2,1,0:T(8,128)S(1)} %get-tuple-element.118.refs_1_.refs_5_) | copy-start | bytes 3145732
  58.1 36.5 %copy-start.4 = (f32[264,256]{1,0:T(8,128)}, f32[264,256]{1,0:T(8,128)S(1)}, u32[]{:S(2)}) copy-start(f32[264,256]{1,0:T(8,128)S(1)} %get-tuple-element.117.refs_1_) | copy-start | bytes 811012
  58.2 11.8 %collective-permute-start.10 = (f32[264,256]{1,0:T(8,128)S(1)}, f32[264,256]{1,0:T(8,128)S(1)}, u32[]{:S(2)}, u32[]{:S(2)}) collective-permute-start(f32[264,256]{1,0:T(8,128)S(1)} %get-tuple-element.117.refs_1_), channel_id=1, source_target_pairs={{0,64},{32,96},{64,0},{96,32},{1,65},{33,97},{65,1},{97,33},{2,66}... | collective-permute-start | bytes 811016 | tf_op jit(solution)/shard_map/ppermute | solution.py:445
  62.6 13.2 %collective-permute-start.9 = (f32[264,256]{1,0:T(8,128)S(1)}, f32[264,256]{1,0:T(8,128)S(1)}, u32[]{:S(2)}, u32[]{:S(2)}) collective-permute-start(f32[264,256]{1,0:T(8,128)S(1)} %get-tuple-element.117.refs_1_), channel_id=1, source_target_pairs={{0,96},{32,0},{64,32},{96,64},{1,97},{33,1},{65,33},{97,65},{2,98}... | collective-permute-start | bytes 811016 | tf_op jit(solution)/shard_map/ppermute | solution.py:445
  63.7 12.1 %collective-permute-start.8 = (f32[264,256]{1,0:T(8,128)S(1)}, f32[264,256]{1,0:T(8,128)S(1)}, u32[]{:S(2)}, u32[]{:S(2)}) collective-permute-start(f32[264,256]{1,0:T(8,128)S(1)} %get-tuple-element.117.refs_1_), channel_id=1, source_target_pairs={{0,32},{32,64},{64,96},{96,0},{1,33},{33,65},{65,97},{97,1},{2,34}... | collective-permute-start | bytes 811016 | tf_op jit(solution)/shard_map/ppermute | solution.py:445
  67.4 0.7 copy-start.9
  68.1 0.7 copy-start.10
  70.0 24.7 %copy-start.5 = (f32[264,256]{1,0:T(8,128)}, f32[264,256]{1,0:T(8,128)S(1)}, u32[]{:S(2)}) copy-start(f32[264,256]{1,0:T(8,128)S(1)} %collective-permute-done.10.refs_4_) | copy-start | bytes 811012
  75.8 18.9 %copy-start.6 = (f32[264,256]{1,0:T(8,128)}, f32[264,256]{1,0:T(8,128)S(1)}, u32[]{:S(2)}) copy-start(f32[264,256]{1,0:T(8,128)S(1)} %collective-permute-done.9.refs_3_) | copy-start | bytes 811012
  75.8 18.9 %copy-start.7 = (f32[264,256]{1,0:T(8,128)}, f32[264,256]{1,0:T(8,128)S(1)}, u32[]{:S(2)}) copy-start(f32[264,256]{1,0:T(8,128)S(1)} %collective-permute-done.8.refs_2_) | copy-start | bytes 811012
  78.1 18.1 %all-to-all-start = ((f32[64,1,384]{2,1,0:T(1,128)}), f32[64,1,384]{2,1,0:T(1,128)S(1)}, u32[]{:S(2)}, u32[]{:S(2)}) async-start(f32[64,1,384]{2,1,0:T(1,128)} %get-tuple-element.137), calls=%async_computation | async-start | bytes 196608 | tf_op jit(solution)/shard_map/all_to_all | solution.py:553

commit v3 on v2

--- a/solution.py
+++ b/solution.py
@@ -352,18 +352,21 @@
         for j, m in ((1, quad_ref[0]), (2, half_ref[...]), (3, third_ref[...]))
     ]
     ready(1)
+    ready(2)
     for m in range(4):
+        steps = [None] * 4
         for j in range(4):
             k = 4 * j + m
             step = entries[j] - defect_ref[k:k + 1, :]
+            steps[j] = step
             ss_ref[k:k + 1, :] = step
             if m < 3:
                 entries[j] = vec_mat(step, a_ref[k], 1) + push_ref[k:k + 1, :]
-    ready(2)
-    for k in range(16):
-        step = ss_ref[k:k + 1, :]
-        ms_ref[k:k + 1, :] = vec_mat(step - defect_ref[k:k + 1, :], v_ref[k]) + before_ref[k:k + 1, :]
-        is_ref[k:k + 1, :] = vec_mat(step, k_ref[k], 1) + gain_ref[k:k + 1, :]
+        for j in range(4):
+            k = 4 * j + m
+            step = steps[j]
+            ms_ref[k:k + 1, :] = vec_mat(step - defect_ref[k:k + 1, :], v_ref[k]) + before_ref[k:k + 1, :]
+            is_ref[k:k + 1, :] = vec_mat(step, k_ref[k], 1) + gain_ref[k:k + 1, :]
     chosen = active_ref[...].astype(F32)
     step = (1.0 - chosen) * is_ref[...] + chosen * (ub_ref[...] - u_ref[...])
     is_ref[...] = step

time: 104 us -> 105 us (level)
  no operation moved by 1% of the time
where the time goes in v3:
time: 105 us; the launch traced here: 104 us
  Pallas kernels  45.6 us (43%)
  starting transfers between devices  34.1 us (32%)
  waiting for transfers between devices  21.4 us (20%)
  local copies, waits for them, and re-layouts  2.17 us (2%)
  between operations  1.1 us (1%)
    pallas_call x10, Pallas kernels, call(): pl.pallas_call(kernel, in_specs=[SCALARS] * ns + [pl.BlockSpec(memory_spa...  40.1 us
    ppermute x9, waiting for transfers between devices, move(): return lax.ppermute(x, axis, [(i, (i + by) % 4) for i in range(4)])  19.9 us
    ppermute x9, starting transfers between devices, move(): return lax.ppermute(x, axis, [(i, (i + by) % 4) for i in range(4)])  19.7 us
    all_to_all x1, starting transfers between devices, local(): received = lax.all_to_all(message, TM, 0, 0, tiled=True)  8.59 us
    ppermute x2, starting transfers between devices, shifted(): return lax.ppermute(x, TM, pairs)  5.84 us
    pallas_call x1, Pallas kernels, local(): pl.pallas_call(functools.partial(block_product_body, sections=sections, r...  5.55 us
  transfers between devices with their start and end apart: 12, of which 5 were waited for; matrix products, arithmetic and copies ran while one was open for 0% of the time, Pallas kernels for 26%

profile of v3, /device:TPU:0, one launch (start us, length us, event | category | flops | bytes accessed | tf_op | source)
XLA Modules:
  0.0 104.5 jit_solution(7163499659335580708)
XLA Ops:
  0.6 0.7 slice.3
  1.3 0.1 pad_add_fusion.refs_0_
  1.4 1.3 %collective-permute-start.1 = (f32[8,256]{1,0:T(8,128)S(1)}, f32[8,256]{1,0:T(8,128)S(1)}, u32[]{:S(2)}, u32[]{:S(2)}) collective-permute-start(f32[8,256]{1,0:T(8,128)S(1)} %slice.3), channel_id=1, source_target_pairs={{2,0},{4,2},{6,4},{8,6},{10,8},{12,10},{14,12},{16,14},{18,16},{20... | collective-permute-start | bytes 24584 | tf_op jit(solution)/shard_map/ppermute | solution.py:455
  2.7 1.2 %shard_map.200 = f32[8,256]{1,0:T(8,128)S(1)} custom-call(f32[16,256,256]{2,1,0:T(8,128)} %refs_1_.4, f32[16,64,256]{2,1,0:T(8,128)} %refs_2_.5, f32[16,256]{1,0:T(8,128)} %refs_6_.1, f32[16,64]{1,0:T(8,128)} %refs_17_.1), custom_call_target="tpu_custom_call" | custom-call | tf_op jit(solution)/shard_map/pallas_call | solution.py:432
  3.9 4.6 %collective-permute-start = (f32[8,256]{1,0:T(8,128)S(1)}, f32[8,256]{1,0:T(8,128)S(1)}, u32[]{:S(2)}, u32[]{:S(2)}) collective-permute-start(f32[8,256]{1,0:T(8,128)S(1)} %shard_map.200), channel_id=1, source_target_pairs={{0,2},{2,4},{4,6},{6,8},{8,10},{10,12},{12,14},{14,16},{16,18},{18... | collective-permute-start | bytes 24584 | tf_op jit(solution)/shard_map/ppermute | solution.py:455
  8.5 5.5 %block_product.1 = (f32[256,256]{1,0:T(8,128)S(1)}, f32[4,256,256]{2,1,0:T(8,128)S(1)}, f32[4,256,256]{2,1,0:T(8,128)S(1)}, f32[256,256]{1,0:T(8,128)S(1)}, f32[...) custom-call(f32[16,256,256]{2,1,0:T(8,128)} %refs_12_.3, ...), custom_call_target="tpu_custom_call" | custom-call | tf_op jit(solution)/shard_map/block_product/pallas_call | solution.py:495
  14.1 0.0 collective-permute-done.1.refs_19_
  14.1 0.0 collective-permute-done.refs_18_
  14.1 5.5 %shard_map.201 = (f32[16,256]{1,0:T(8,128)S(1)}, f32[16,64]{1,0:T(8,128)S(1)}, f32[16,256]{1,0:T(8,128)S(1)}, f32[16,256]{1,0:T(8,128)S(1)}, f32[264,256]{1,0:T(8,128)S(1)}, /*index=5*/f32[8,128]{1,0:T(8,128)S(1)}) custom-call(f32[16,256,256]{2,1,0:T(8,128)S(1)} %get-tuple-element.76.refs_0_, f32[16,64,256]{2,1,0:T(8,128)S(1)} %get-tuple-element.77.refs_1_, ...), custom_call_target="tpu_custom_call" | custom-call | tf_op jit(solution)/shard_map/pallas_call | solution.py:432
  19.6 0.0 copy-start.11
  19.6 0.0 copy-start.12
  19.6 0.0 copy-start.13
  19.6 0.0 copy-start.14
  19.6 4.1 %collective-permute-start.4 = (f32[264,256]{1,0:T(8,128)S(1)}, f32[264,256]{1,0:T(8,128)S(1)}, u32[]{:S(2)}, u32[]{:S(2)}) collective-permute-start(f32[264,256]{1,0:T(8,128)S(1)} %get-tuple-element.98.refs_1_), channel_id=1, source_target_pairs={{0,4},{2,6},{4,0},{6,2},{1,5},{3,7},{5,1},{7,3},{8,12},{10,14},{12... | collective-permute-start | bytes 811016 | tf_op jit(solution)/shard_map/ppermute | solution.py:448
  23.7 2.4 %collective-permute-start.3 = (f32[264,256]{1,0:T(8,128)S(1)}, f32[264,256]{1,0:T(8,128)S(1)}, u32[]{:S(2)}, u32[]{:S(2)}) collective-permute-start(f32[264,256]{1,0:T(8,128)S(1)} %get-tuple-element.98.refs_1_), channel_id=1, source_target_pairs={{0,6},{2,0},{4,2},{6,4},{1,7},{3,1},{5,3},{7,5},{8,14},{10,8},{12,... | collective-permute-start | bytes 811016 | tf_op jit(solution)/shard_map/ppermute | solution.py:448
  26.0 0.8 collective-permute-start.2
  26.8 4.2 %shard_map.202 = (f32[256,256]{1,0:T(8,128)S(1)}, f32[256,256]{1,0:T(8,128)S(1)}) custom-call(f32[16,256,256]{2,1,0:T(8,128)S(1)} %get-tuple-element.80.refs_4_.refs_0_, f32[16,64,256]{2,1,0:T(8,128)S(1)} %get-tuple-element.77.refs_1_, f32[16,64,64]{2,1,0:T(8,128)S(1)} %get-tuple-element.99.refs_2_, f32[4,256,256]{2,1,0:T(8,128)S(1)} %get-tuple-element.100.refs_3_, ...), custom_call_target="tpu_custom_call" | custom-call | tf_op jit(solution)/shard_map/pallas_call | solution.py:432
  31.0 0.0 collective-permute-done.4.refs_4_
  31.1 7.2 %collective-permute-done.3.refs_3_ = f32[264,256]{1,0:T(8,128)S(1)} collective-permute-done((f32[264,256]{1,0:T(8,128)S(1)}, f32[264,256]{1,0:T(8,128)S(1)}, u32[]{:S(2)}, u32[]{:S(2)}) %collective-permute-start.3) | collective-permute-done | bytes 270368 | tf_op jit(solution)/shard_map/ppermute | solution.py:448
  38.3 0.0 collective-permute-done.2.refs_2_
  38.3 1.6 %shard_map.203 = (f32[4,256,256]{2,1,0:T(8,128)S(1)}, f32[4,8,256]{2,1,0:T(8,128)S(1)}, f32[264,256]{1,0:T(8,128)S(1)}) custom-call(s32[3]{0:T(128)S(1)} %pad_add_fusion.refs_0_, f32[264,256]{1,0:T(8,128)S(1)} %get-tuple-element.98.refs_1_, f32[264,256]{1,0:T(8,128)S(1)} %collective-permute-done.2.refs_2_, f32[264,256]{1,0:T(8,128)S(1)} %collective-permute-done.3.refs_3_, ...), custom_call_target="tpu_custom_call" | custom-call | tf_op jit(solution)/shard_map/pallas_call | solution.py:432
  39.9 3.3 %collective-permute-start.7 = (f32[264,256]{1,0:T(8,128)S(1)}, f32[264,256]{1,0:T(8,128)S(1)}, u32[]{:S(2)}, u32[]{:S(2)}) collective-permute-start(f32[264,256]{1,0:T(8,128)S(1)} %get-tuple-element.107.refs_1_), channel_id=1, source_target_pairs={{0,16},{8,24},{16,0},{24,8},{1,17},{9,25},{17,1},{25,9},{2,18},{10... | collective-permute-start | bytes 811016 | tf_op jit(solution)/shard_map/ppermute | solution.py:448
  43.1 1.9 %collective-permute-start.6 = (f32[264,256]{1,0:T(8,128)S(1)}, f32[264,256]{1,0:T(8,128)S(1)}, u32[]{:S(2)}, u32[]{:S(2)}) collective-permute-start(f32[264,256]{1,0:T(8,128)S(1)} %get-tuple-element.107.refs_1_), channel_id=1, source_target_pairs={{0,24},{8,0},{16,8},{24,16},{1,25},{9,1},{17,9},{25,17},{2,26},{10... | collective-permute-start | bytes 811016 | tf_op jit(solution)/shard_map/ppermute | solution.py:448
  45.1 0.8 collective-permute-start.5
  45.8 0.0 copy-done.11
  45.9 5.1 %shard_map.204.refs_9_ = f32[8,256]{1,0:T(8,128)S(1)} custom-call(f32[16,256,256]{2,1,0:T(8,128)S(1)} %get-tuple-element.80.refs_4_.refs_0_, f32[16,64,256]{2,1,0:T(8,128)S(1)} %get-tuple-element.77.refs_1_, f32[16,64,64]{2,1,0:T(8,128)S(1)} %get-tuple-element.99.refs_2_, f32[4,256,256]{2,1,0:T(8,128)S(1)} %get-tuple-element.91.refs_15_.refs_4_.refs_3_.refs_0_.refs_9_, ...), custom_call_target="tpu_custom_call" | custom-call | tf_op jit(solution)/shard_map/pallas_call | solution.py:432
  50.9 0.0 collective-permute-done.7.refs_4_
  51.0 5.6 %collective-permute-done.6.refs_3_ = f32[264,256]{1,0:T(8,128)S(1)} collective-permute-done((f32[264,256]{1,0:T(8,128)S(1)}, f32[264,256]{1,0:T(8,128)S(1)}, u32[]{:S(2)}, u32[]{:S(2)}) %collective-permute-start.6) | collective-permute-done | bytes 270368 | tf_op jit(solution)/shard_map/ppermute | solution.py:448
  56.6 0.0 collective-permute-done.5.refs_2_
  56.6 1.6 %shard_map.205 = (f32[4,256,256]{2,1,0:T(8,128)S(1)}, f32[4,8,256]{2,1,0:T(8,128)S(1)}, f32[264,256]{1,0:T(8,128)S(1)}) custom-call(s32[3]{0:T(128)S(1)} %pad_add_fusion.refs_0_, f32[264,256]{1,0:T(8,128)S(1)} %get-tuple-element.107.refs_1_, f32[264,256]{1,0:T(8,128)S(1)} %collective-permute-done.5.refs_2_, f32[264,256]{1,0:T(8,128)S(1)} %collective-permute-done.6.refs_3_, ...), custom_call_target="tpu_custom_call" | custom-call | tf_op jit(solution)/shard_map/pallas_call | solution.py:432
  58.2 4.5 %collective-permute-start.10 = (f32[264,256]{1,0:T(8,128)S(1)}, f32[264,256]{1,0:T(8,128)S(1)}, u32[]{:S(2)}, u32[]{:S(2)}) collective-permute-start(f32[264,256]{1,0:T(8,128)S(1)} %get-tuple-element.117.refs_1_), channel_id=1, source_target_pairs={{0,64},{32,96},{64,0},{96,32},{1,65},{33,97},{65,1},{97,33},{2,66}... | collective-permute-start | bytes 811016 | tf_op jit(solution)/shard_map/ppermute | solution.py:448
  62.6 1.1 %collective-permute-start.9 = (f32[264,256]{1,0:T(8,128)S(1)}, f32[264,256]{1,0:T(8,128)S(1)}, u32[]{:S(2)}, u32[]{:S(2)}) collective-permute-start(f32[264,256]{1,0:T(8,128)S(1)} %get-tuple-element.117.refs_1_), channel_id=1, source_target_pairs={{0,96},{32,0},{64,32},{96,64},{1,97},{33,1},{65,33},{97,65},{2,98}... | collective-permute-start | bytes 811016 | tf_op jit(solution)/shard_map/ppermute | solution.py:448
  63.7 1.0 collective-permute-start.8
  64.6 2.7 %shard_map.206 = (f32[256,256]{1,0:T(8,128)S(1)}, f32[256,256]{1,0:T(8,128)S(1)}, f32[8,256]{1,0:T(8,128)S(1)}, f32[256,256]{1,0:T(8,128)S(1)}, f32[256,256]{1,0:T(8,128)S(1)}) custom-call(s32[3]{0:T(128)S(1)} %pad_add_fusion.refs_0_, f32[4,256,256]{2,1,0:T(8,128)S(1)} %get-tuple-element.118.refs_1_.refs_5_, f32[4,8,256]{2,1,0:T(8,128)S(1)} %get-tuple-element.120.refs_2_, ...), custom_call_target="tpu_custom_call" | custom-call | tf_op jit(solution)/shard_map/pallas_call | solution.py:432
  67.4 0.7 copy-done.9
  68.1 0.7 copy-done.10
  68.8 1.2 %collective-permute-done.10.refs_4_ = f32[264,256]{1,0:T(8,128)S(1)} collective-permute-done((f32[264,256]{1,0:T(8,128)S(1)}, f32[264,256]{1,0:T(8,128)S(1)}, u32[]{:S(2)}, u32[]{:S(2)}) %collective-permute-start.10) | collective-permute-done | bytes 270368 | tf_op jit(solution)/shard_map/ppermute | solution.py:448
  70.0 5.8 %collective-permute-done.9.refs_3_ = f32[264,256]{1,0:T(8,128)S(1)} collective-permute-done((f32[264,256]{1,0:T(8,128)S(1)}, f32[264,256]{1,0:T(8,128)S(1)}, u32[]{:S(2)}, u32[]{:S(2)}) %collective-permute-start.9) | collective-permute-done | bytes 270368 | tf_op jit(solution)/shard_map/ppermute | solution.py:448
  75.8 0.0 collective-permute-done.8.refs_2_
  75.8 2.3 %shard_map.207 = (f32[8,256]{1,0:T(8,128)}, f32[64,1,384]{2,1,0:T(1,128)}) custom-call(s32[3]{0:T(128)S(1)} %pad_add_fusion.refs_0_, f32[264,256]{1,0:T(8,128)S(1)} %get-tuple-element.117.refs_1_, f32[264,256]{1,0:T(8,128)S(1)} %collective-permute-done.8.refs_2_, f32[264,256]{1,0:T(8,128)S(1)} %collective-permute-done.9.refs_3_, ...), custom_call_target="tpu_custom_call" | custom-call | tf_op jit(solution)/shard_map/pallas_call | solution.py:432
  78.1 8.6 %all-to-all-start = ((f32[64,1,384]{2,1,0:T(1,128)}), f32[64,1,384]{2,1,0:T(1,128)S(1)}, u32[]{:S(2)}, u32[]{:S(2)}) async-start(f32[64,1,384]{2,1,0:T(1,128)} %get-tuple-element.137), calls=%async_computation | async-start | bytes 196608 | tf_op jit(solution)/shard_map/all_to_all | solution.py:556
  86.7 8.0 %shard_map.208 = (f32[16,256]{1,0:T(8,128)}, f32[16,64]{1,0:T(8,128)}, f32[16,64]{1,0:T(8,128)}, f32[16,256]{1,0:T(8,128)}, f32[8,256]{1,0:T(8,128)}) custom-call(f32[4,256,256]{2,1,0:T(8,128)} %copy-done, f32[16,256,256]{2,1,0:T(8,128)} %refs_12_.3, f32[16,64,256]{2,1,0:T(8,128)} %refs_2_.5, f32[16,64,64]{2,1,0:T(8,128)} %refs_3_.5, f32[16,256]{1,0:T(8,128)} %copy-done.13, ...), custom_call_target="tpu_custom_call" | custom-call | tf_op jit(solution)/shard_map/pallas_call | solution.py:432
  94.7 0.0 copy-done.2
  94.7 0.0 copy-done.4
  94.7 0.0 copy-done.5
  94.7 0.0 copy-done.6
  94.7 1.5 %all-to-all-done.refs_25_ = f32[64,1,384]{2,1,0:T(1,128)S(1)} async-done(((f32[64,1,384]{2,1,0:T(1,128)}), f32[64,1,384]{2,1,0:T(1,128)S(1)}, u32[]{:S(2)}, u32[]{:S(2)}) %all-to-all-start) | async-done | bytes 98336 | tf_op jit(solution)/shard_map/all_to_all | solution.py:556
  96.2 8.1 %shard_map.209 = (f32[16,256]{1,0:T(8,128)}, f32[16,64]{1,0:T(8,128)}, f32[16,256]{1,0:T(8,128)}, f32[16,64]{1,0:T(8,128)}, f32[1,3]{1,0:T(1,128)}) custom-call(s32[3]{0:T(128)S(1)} %pad_add_fusion.refs_0_, f32[264,256]{1,0:T(8,128)} %copy-done.4, f32[264,256]{1,0:T(8,128)} %copy-done.7, f32[264,256]{1,0:T(8,128)} %copy-done.6, f32[264,256]{1,0:T(8,128)} %copy-done.5, ...), custom_call_target="tpu_custom_call" | custom-call | tf_op jit(solution)/shard_map/pallas_call | solution.py:432
  (19 shorter events, 0.0 us)
Async XLA Ops:
  1.4 12.6 %collective-permute-start.1 = (f32[8,256]{1,0:T(8,128)S(1)}, f32[8,256]{1,0:T(8,128)S(1)}, u32[]{:S(2)}, u32[]{:S(2)}) collective-permute-start(f32[8,256]{1,0:T(8,128)S(1)} %slice.3), channel_id=1, source_target_pairs={{2,0},{4,2},{6,4},{8,6},{10,8},{12,10},{14,12},{16,14},{18,16},{20... | collective-permute-start | bytes 24584 | tf_op jit(solution)/shard_map/ppermute | solution.py:455
  3.9 10.2 %collective-permute-start = (f32[8,256]{1,0:T(8,128)S(1)}, f32[8,256]{1,0:T(8,128)S(1)}, u32[]{:S(2)}, u32[]{:S(2)}) collective-permute-start(f32[8,256]{1,0:T(8,128)S(1)} %shard_map.200), channel_id=1, source_target_pairs={{0,2},{2,4},{4,6},{6,8},{8,10},{10,12},{12,14},{14,16},{16,18},{18... | collective-permute-start | bytes 24584 | tf_op jit(solution)/shard_map/ppermute | solution.py:455
  14.0 12.8 %copy-start.3 = (f32[256,256]{1,0:T(8,128)}, f32[256,256]{1,0:T(8,128)S(1)}, u32[]{:S(2)}) copy-start(f32[256,256]{1,0:T(8,128)S(1)} %get-tuple-element.92.refs_16_.refs_5_.refs_10_) | copy-start | bytes 786436
  14.0 31.8 %copy-start = (f32[4,256,256]{2,1,0:T(8,128)}, f32[4,256,256]{2,1,0:T(8,128)S(1)}, u32[]{:S(2)}) copy-start(f32[4,256,256]{2,1,0:T(8,128)S(1)} %get-tuple-element.91.refs_15_.refs_4_.refs_3_.refs_0_.refs_9_) | copy-start | bytes 3145732
  19.6 26.3 %copy-start.11 = (f32[16,256]{1,0:T(8,128)}, f32[16,256]{1,0:T(8,128)S(1)}, u32[]{:S(2)}) copy-start(f32[16,256]{1,0:T(8,128)S(1)} %get-tuple-element.111.refs_7_.refs_19_) | copy-start | bytes 49156
  19.6 26.3 %copy-start.12 = (f32[16,256]{1,0:T(8,128)}, f32[16,256]{1,0:T(8,128)S(1)}, u32[]{:S(2)}) copy-start(f32[16,256]{1,0:T(8,128)S(1)} %get-tuple-element.109.refs_5_) | copy-start | bytes 49156
  19.6 26.3 %copy-start.13 = (f32[16,256]{1,0:T(8,128)}, f32[16,256]{1,0:T(8,128)S(1)}, u32[]{:S(2)}) copy-start(f32[16,256]{1,0:T(8,128)S(1)} %get-tuple-element.108.refs_4_) | copy-start | bytes 49156
  19.6 26.3 %copy-start.14 = (f32[16,64]{1,0:T(8,128)}, f32[16,64]{1,0:T(8,128)S(1)}, u32[]{:S(2)}) copy-start(f32[16,64]{1,0:T(8,128)S(1)} %get-tuple-element.110.refs_6_) | copy-start | bytes 12292
  19.6 11.4 %collective-permute-start.4 = (f32[264,256]{1,0:T(8,128)S(1)}, f32[264,256]{1,0:T(8,128)S(1)}, u32[]{:S(2)}, u32[]{:S(2)}) collective-permute-start(f32[264,256]{1,0:T(8,128)S(1)} %get-tuple-element.98.refs_1_), channel_id=1, source_target_pairs={{0,4},{2,6},{4,0},{6,2},{1,5},{3,7},{5,1},{7,3},{8,12},{10,14},{12... | collective-permute-start | bytes 811016 | tf_op jit(solution)/shard_map/ppermute | solution.py:448
  23.7 14.6 %collective-permute-start.3 = (f32[264,256]{1,0:T(8,128)S(1)}, f32[264,256]{1,0:T(8,128)S(1)}, u32[]{:S(2)}, u32[]{:S(2)}) collective-permute-start(f32[264,256]{1,0:T(8,128)S(1)} %get-tuple-element.98.refs_1_), channel_id=1, source_target_pairs={{0,6},{2,0},{4,2},{6,4},{1,7},{3,1},{5,3},{7,5},{8,14},{10,8},{12,... | collective-permute-start | bytes 811016 | tf_op jit(solution)/shard_map/ppermute | solution.py:448
  26.0 12.3 %collective-permute-start.2 = (f32[264,256]{1,0:T(8,128)S(1)}, f32[264,256]{1,0:T(8,128)S(1)}, u32[]{:S(2)}, u32[]{:S(2)}) collective-permute-start(f32[264,256]{1,0:T(8,128)S(1)} %get-tuple-element.98.refs_1_), channel_id=1, source_target_pairs={{0,2},{2,4},{4,6},{6,0},{1,3},{3,5},{5,7},{7,1},{8,10},{10,12},{12... | collective-permute-start | bytes 811016 | tf_op jit(solution)/shard_map/ppermute | solution.py:448
  31.0 8.8 %copy-start.8 = (f32[256,256]{1,0:T(8,128)}, f32[256,256]{1,0:T(8,128)S(1)}, u32[]{:S(2)}) copy-start(f32[256,256]{1,0:T(8,128)S(1)} %get-tuple-element.124.refs_11_) | copy-start | bytes 786436
  39.8 27.5 %copy-start.1 = (f32[4,256,256]{2,1,0:T(8,128)}, f32[4,256,256]{2,1,0:T(8,128)S(1)}, u32[]{:S(2)}) copy-start(f32[4,256,256]{2,1,0:T(8,128)S(1)} %get-tuple-element.119.refs_3_.refs_6_) | copy-start | bytes 3145732
  39.9 11.1 %collective-permute-start.7 = (f32[264,256]{1,0:T(8,128)S(1)}, f32[264,256]{1,0:T(8,128)S(1)}, u32[]{:S(2)}, u32[]{:S(2)}) collective-permute-start(f32[264,256]{1,0:T(8,128)S(1)} %get-tuple-element.107.refs_1_), channel_id=1, source_target_pairs={{0,16},{8,24},{16,0},{24,8},{1,17},{9,25},{17,1},{25,9},{2,18},{10... | collective-permute-start | bytes 811016 | tf_op jit(solution)/shard_map/ppermute | solution.py:448
  43.1 13.4 %collective-permute-start.6 = (f32[264,256]{1,0:T(8,128)S(1)}, f32[264,256]{1,0:T(8,128)S(1)}, u32[]{:S(2)}, u32[]{:S(2)}) collective-permute-start(f32[264,256]{1,0:T(8,128)S(1)} %get-tuple-element.107.refs_1_), channel_id=1, source_target_pairs={{0,24},{8,0},{16,8},{24,16},{1,25},{9,1},{17,9},{25,17},{2,26},{10... | collective-permute-start | bytes 811016 | tf_op jit(solution)/shard_map/ppermute | solution.py:448
  45.1 11.5 %collective-permute-start.5 = (f32[264,256]{1,0:T(8,128)S(1)}, f32[264,256]{1,0:T(8,128)S(1)}, u32[]{:S(2)}, u32[]{:S(2)}) collective-permute-start(f32[264,256]{1,0:T(8,128)S(1)} %get-tuple-element.107.refs_1_), channel_id=1, source_target_pairs={{0,8},{8,16},{16,24},{24,0},{1,9},{9,17},{17,25},{25,1},{2,10},{10... | collective-permute-start | bytes 811016 | tf_op jit(solution)/shard_map/ppermute | solution.py:448
  58.1 36.5 %copy-start.2 = (f32[4,256,256]{2,1,0:T(8,128)}, f32[4,256,256]{2,1,0:T(8,128)S(1)}, u32[]{:S(2)}) copy-start(f32[4,256,256]{2,1,0:T(8,128)S(1)} %get-tuple-element.118.refs_1_.refs_5_) | copy-start | bytes 3145732
  58.1 36.5 %copy-start.4 = (f32[264,256]{1,0:T(8,128)}, f32[264,256]{1,0:T(8,128)S(1)}, u32[]{:S(2)}) copy-start(f32[264,256]{1,0:T(8,128)S(1)} %get-tuple-element.117.refs_1_) | copy-start | bytes 811012
  58.2 11.8 %collective-permute-start.10 = (f32[264,256]{1,0:T(8,128)S(1)}, f32[264,256]{1,0:T(8,128)S(1)}, u32[]{:S(2)}, u32[]{:S(2)}) collective-permute-start(f32[264,256]{1,0:T(8,128)S(1)} %get-tuple-element.117.refs_1_), channel_id=1, source_target_pairs={{0,64},{32,96},{64,0},{96,32},{1,65},{33,97},{65,1},{97,33},{2,66}... | collective-permute-start | bytes 811016 | tf_op jit(solution)/shard_map/ppermute | solution.py:448
  62.6 13.2 %collective-permute-start.9 = (f32[264,256]{1,0:T(8,128)S(1)}, f32[264,256]{1,0:T(8,128)S(1)}, u32[]{:S(2)}, u32[]{:S(2)}) collective-permute-start(f32[264,256]{1,0:T(8,128)S(1)} %get-tuple-element.117.refs_1_), channel_id=1, source_target_pairs={{0,96},{32,0},{64,32},{96,64},{1,97},{33,1},{65,33},{97,65},{2,98}... | collective-permute-start | bytes 811016 | tf_op jit(solution)/shard_map/ppermute | solution.py:448
  63.7 12.1 %collective-permute-start.8 = (f32[264,256]{1,0:T(8,128)S(1)}, f32[264,256]{1,0:T(8,128)S(1)}, u32[]{:S(2)}, u32[]{:S(2)}) collective-permute-start(f32[264,256]{1,0:T(8,128)S(1)} %get-tuple-element.117.refs_1_), channel_id=1, source_target_pairs={{0,32},{32,64},{64,96},{96,0},{1,33},{33,65},{65,97},{97,1},{2,34}... | collective-permute-start | bytes 811016 | tf_op jit(solution)/shard_map/ppermute | solution.py:448
  67.4 0.7 copy-start.9
  68.1 0.7 copy-start.10
  70.0 24.7 %copy-start.5 = (f32[264,256]{1,0:T(8,128)}, f32[264,256]{1,0:T(8,128)S(1)}, u32[]{:S(2)}) copy-start(f32[264,256]{1,0:T(8,128)S(1)} %collective-permute-done.10.refs_4_) | copy-start | bytes 811012
  75.8 18.9 %copy-start.6 = (f32[264,256]{1,0:T(8,128)}, f32[264,256]{1,0:T(8,128)S(1)}, u32[]{:S(2)}) copy-start(f32[264,256]{1,0:T(8,128)S(1)} %collective-permute-done.9.refs_3_) | copy-start | bytes 811012
  75.8 18.9 %copy-start.7 = (f32[264,256]{1,0:T(8,128)}, f32[264,256]{1,0:T(8,128)S(1)}, u32[]{:S(2)}) copy-start(f32[264,256]{1,0:T(8,128)S(1)} %collective-permute-done.8.refs_2_) | copy-start | bytes 811012
  78.1 18.1 %all-to-all-start = ((f32[64,1,384]{2,1,0:T(1,128)}), f32[64,1,384]{2,1,0:T(1,128)S(1)}, u32[]{:S(2)}, u32[]{:S(2)}) async-start(f32[64,1,384]{2,1,0:T(1,128)} %get-tuple-element.137), calls=%async_computation | async-start | bytes 196608 | tf_op jit(solution)/shard_map/all_to_all | solution.py:556
